TPU v7x, 32 devices: a whole 2x2x4 slice. The times are simulated.
32 devices in a mesh: pix: 32 (over z, y, x, core).
Axes of the slice: x: 2, y: 2, z: 4, core: 2. Of those that a mesh axis runs over, the one named last changes fastest.
Arguments:
- green: float32 [2048, 6144], P('pix'), may hold values from -200 to 200, as said below
- sketch: float32 [6144, 128], P('pix'), may hold values from -0.078125 to 0.078125
Outputs:
- basis: float32 [2048, 128], P('pix')
- projection: float32 [6144, 128], P('pix')
- spectrum_gram: float32 [128, 128], replicated
Inputs may be any that keep to these rules, and one draw needn't show every extreme that they name: `green`: finite real entries; each patch's column has its own scale.
All inputs are finite; a program needn't handle non-finite values.
Results may differ from a plain program's by a relative error of at most 0.000086.
Values sent between devices are 32-bit elements; how exact they have to be, the bound alone decides.
No kernel may reach another device: no remote copies, remote signals or barrier semaphores. Data moves between devices by JAX's collectives and lax.ppermute only.
A program may use at most 64 MiB of HBM per device.

v0:
```python
import jax
import jax.numpy as jnp
from jax import lax
from jax.sharding import PartitionSpec as P

PATCHES = 6144


def body(green, sketch):
    highest = lax.Precision.HIGHEST
    rows_here = green.shape[0]
    devices_pix = lax.axis_size("pix")
    total_pixels = rows_here * devices_pix
    columns = green
    sketched = jnp.dot(
        columns,
        lax.all_gather(sketch, "pix", axis=0, tiled=True),
        precision=highest,
        preferred_element_type=jnp.float32,
    )
    local_gram = jnp.dot(
        sketched.T, sketched, precision=highest, preferred_element_type=jnp.float32
    )
    columns = green
    raw_proj = lax.psum_scatter(
        lax.dot_general(
            columns,
            sketched,
            (((0,), (0,)), ((), ())),
            precision=highest,
            preferred_element_type=jnp.float32,
        ),
        "pix",
        scatter_dimension=0,
        tiled=True,
    )
    gram = lax.psum(local_gram, "pix")
    lower = jnp.linalg.cholesky(gram)
    orthonormal = jax.scipy.linalg.solve_triangular(lower, sketched.T, lower=True).T
    projection = jax.scipy.linalg.solve_triangular(lower, raw_proj.T, lower=True).T
    basis = jnp.sqrt(jnp.float32(total_pixels)) * orthonormal
    local_spec = jnp.dot(
        projection.T, projection, precision=highest, preferred_element_type=jnp.float32
    )
    spectrum_gram = lax.psum(local_spec, "pix") / jnp.float32(PATCHES)
    return (basis, projection, spectrum_gram)


def solution(mesh):
    in_specs = (P("pix", None), P("pix", None))
    out_specs = (P("pix", None), P("pix", None), P())
    return jax.shard_map(body, mesh=mesh, in_specs=in_specs, out_specs=out_specs, check_vma=False)
```

profile of v0, /device:TPU:0, one launch (start us, length us, event | category | flops | bytes accessed | tf_op | source)
XLA Modules:
  0.0 438.3 jit_solution(5103394524616839399)
XLA Ops:
  7.2 0.0 copy-start
  7.2 0.0 all-gather.2.cloned.1.call-start
  7.2 0.7 all-gather.2.cloned.1.call-update
  7.9 0.0 all-reduce.3.cloned.1.call-start
  8.0 64.7 %all-gather.2.cloned.1.call-done = f32[6144,128]{1,0:T(8,128)} async-done(((f32[192,128]{1,0:T(8,128)}), f32[6144,128]{1,0:T(8,128)}) %all-gather.2.cloned.1.call-update) | async-done | bytes 3145744 | tf_op jit(solution)/shard_map/all_gather | solution.py:17
  72.7 0.0 copy-done
  72.7 3.9 fusion.5
  76.6 0.9 fusion.6
  77.5 0.0 all-reduce.3.cloned.1.call-update
  77.5 0.0 reduce-scatter.4.cloned.1.call-start
  77.6 4.4 convolution_bitcast_fusion
  81.9 3.6 copy.10
  85.5 0.0 reduce-scatter.4.cloned.1.call-update
  85.5 0.2 all-reduce.5.cloned.1.call-start
  85.8 111.2 %all-reduce.3.cloned.1.call-done = f32[128,128]{0,1:T(8,128)} async-done(((f32[128,128]{0,1:T(8,128)}), f32[128,128]{0,1:T(8,128)}) %all-reduce.3.cloned.1.call-update) | async-done | bytes 65552 | tf_op jit(solution)/shard_map/psum | solution.py:37
  197.0 0.9 copy.8
  197.9 0.9 fusion.4
  198.8 11.7 %cholesky.16 = f32[128,128]{1,0:T(8,128)S(1)} custom-call(f32[128,128]{1,0:T(8,128)S(1)} %fusion.4), custom_call_target="Cholesky" | custom-call | tf_op jit(solution)/shard_map/jit(cholesky)/cholesky | solution.py:38
  210.5 0.6 compare_reduce_fusion
  211.1 0.7 fusion
  211.8 9.8 %custom-call.10 = f32[1,128,128]{1,2,0:T(8,128)S(1)} custom-call(f32[1,128,128]{2,1,0:T(8,128)S(1)} %fusion), custom_call_target="InvertDiagBlocksLowerTriangular" | custom-call | tf_op jit(solution)/shard_map/jit(_solve_triangular)/triangular_solve | solution.py:39
  221.6 84.3 %reduce-scatter.4.cloned.1.call-done = f32[192,128]{1,0:T(8,128)} async-done(((f32[6144,128]{1,0:T(8,128)}), f32[192,128]{1,0:T(8,128)}) %reduce-scatter.4.cloned.1.call-update) | async-done | bytes 98320
  305.9 1.1 fusion.1
  307.1 0.0 copy-start.1
  307.1 1.1 fusion.7
  308.2 0.0 all-reduce.5.cloned.1.call-update
  308.2 0.8 convolution_multiply_fusion
  309.0 121.3 %all-reduce.5.cloned.1.call-done = f32[128,128]{1,0:T(8,128)} async-done(((f32[128,128]{1,0:T(8,128)}), f32[128,128]{1,0:T(8,128)}) %all-reduce.5.cloned.1.call-update) | async-done | bytes 65552 | tf_op jit(solution)/shard_map/psum | solution.py:45
  430.3 1.5 broadcast_multiply_fusion
  431.8 0.0 copy-done.1
  (1 shorter events, 0.0 us)
Async XLA Ops:
  7.2 65.5 %copy-start = (f32[64,6144]{1,0:T(8,128)S(1)}, f32[64,6144]{1,0:T(8,128)}, u32[]{:S(2)}) copy-start(f32[64,6144]{1,0:T(8,128)} %param.2) | copy-start | bytes 4718596
  7.2 65.5 %all-gather.2.cloned.1.call-start = ((), (), s32[]{:S(2)}) async-start(), calls=%async_computation.1 | async-start | bytes 3244032 | tf_op jit(solution)/shard_map/all_gather | solution.py:17
  7.9 189.0 %all-reduce.3.cloned.1.call-start = ((), (), s32[]{:S(2)}) async-start(), calls=%async_computation.2 | async-start | bytes 131072 | tf_op jit(solution)/shard_map/psum | solution.py:37
  77.5 228.4 %reduce-scatter.4.cloned.1.call-start = ((), (), s32[]{:S(2)}) async-start(), calls=%async_computation.4 | async-start | bytes 3244032
  85.5 344.8 %all-reduce.5.cloned.1.call-start = ((), (), s32[]{:S(2)}) async-start(), calls=%async_computation.3 | async-start | bytes 131072 | tf_op jit(solution)/shard_map/psum | solution.py:45
  307.1 124.7 %copy-start.1 = (f32[128,192]{0,1:T(8,128)}, f32[128,192]{0,1:T(8,128)S(1)}, u32[]{:S(2)}) copy-start(f32[128,192]{0,1:T(8,128)S(1)} %fusion.1) | copy-start | bytes 294916
Sparse Core Ops, SparseCore 0:
  10.9 61.7 all-gather.1
  78.8 118.0 all-reduce.2
  202.4 103.4 reduce-scatter.3
  311.9 118.3 all-reduce.4
where the time goes:
time: 440 us; the launch traced here: 438 us
  waiting for transfers between devices  382 us (87%)
  other arithmetic  25.2 us (6%)
  between operations  13.8 us (3%)
  matrix products  12.2 us (3%)
  local copies, waits for them, and re-layouts  4.5 us (1%)
    psum x1, waiting for transfers between devices, body(): spectrum_gram = lax.psum(local_spec, 'pix') / jnp.float32(PATCHES)  121 us
    psum x1, waiting for transfers between devices, body(): gram = lax.psum(local_gram, 'pix')  111 us
    unnamed x5, waiting for transfers between devices  85 us
    all_gather x1, waiting for transfers between devices, body(): lax.all_gather(sketch, 'pix', axis=0, tiled=True)  64.7 us
    another operation x3, other arithmetic, body(): lower = jnp.linalg.cholesky(gram)  12.4 us
    another operation x2, other arithmetic, body(): jax.scipy.linalg.solve_triangular(lower, sketched.T, lower=True)  10.5 us
  transfers between devices with their start and end apart: 4, of which 4 were waited for; matrix products, arithmetic and copies ran while one was open for 8% of the time, Pallas kernels for 0%

commit v1 on v0

v1 whole, which is shorter than its diff:
```python
import jax
import jax.numpy as jnp
from jax import lax
from jax.sharding import PartitionSpec as P

HIGHEST = lax.Precision.HIGHEST
HIGH = lax.Precision.HIGH


def dot(a, b, contract, precision=HIGHEST):
    return lax.dot_general(
        a, b, (contract, ((), ())), precision=precision, preferred_element_type=jnp.float32
    )


def strides(n):
    assert n & (n - 1) == 0
    out = []
    s = 1
    while s < n:
        out.append(s)
        s *= 2
    return out


def swap(x, s, n):
    return lax.ppermute(x, "pix", [(i, i ^ s) for i in range(n)])


def gather_rows(x, me, n):
    rows, cols = x.shape
    b = x[None]
    for s in reversed(strides(n)):
        other = swap(b, s, n)
        bit = (me // s) % 2
        low = jnp.where(bit == 0, b, other)
        high = jnp.where(bit == 0, other, b)
        b = jnp.stack([low, high], axis=1).reshape(-1, rows, cols)
    return b.reshape(-1, cols)


def scatter_sum(x, me, n):
    rows, cols = x.shape
    b = x.reshape(n, rows // n, cols)
    for s in strides(n):
        bit = (me // s) % 2
        pairs = b.reshape(-1, 2, rows // n, cols)
        keep = lax.dynamic_index_in_dim(pairs, bit, 1, False)
        send = lax.dynamic_index_in_dim(pairs, 1 - bit, 1, False)
        b = keep + swap(send, s, n)
    return b[0]


def total(x, n):
    for s in strides(n):
        x = x + swap(x, s, n)
    return x


def body(green, sketch):
    n = lax.axis_size("pix")
    me = lax.axis_index("pix")
    total_pixels = green.shape[0] * n
    patches = green.shape[1]
    sketched = dot(green, gather_rows(sketch, me, n), ((1,), (0,)), HIGH)
    gram = total(dot(sketched, sketched, ((0,), (0,))), n)
    raw = scatter_sum(dot(green, sketched, ((0,), (0,)), HIGH), me, n)
    raw_gram = total(dot(raw, raw, ((0,), (0,))), n)
    lower = jnp.linalg.cholesky(gram)
    inverse = jax.scipy.linalg.solve_triangular(
        lower, jnp.eye(lower.shape[0], dtype=jnp.float32), lower=True
    )
    basis = jnp.sqrt(jnp.float32(total_pixels)) * dot(sketched, inverse, ((1,), (1,)))
    projection = dot(raw, inverse, ((1,), (1,)))
    spectrum = dot(dot(inverse, raw_gram, ((1,), (0,))), inverse, ((1,), (1,)))
    return (basis, projection, spectrum / jnp.float32(patches))


def solution(mesh):
    in_specs = (P("pix", None), P("pix", None))
    out_specs = (P("pix", None), P("pix", None), P())
    return jax.shard_map(body, mesh=mesh, in_specs=in_specs, out_specs=out_specs, check_vma=False)
```

time: 440 us -> 163 us (0.37)
  waiting for transfers between devices: 382 us -> 85.3 us
  starting transfers between devices: 0.34 us -> 30.1 us
  between operations: 13.8 us -> 0.97 us
  other arithmetic: 25.2 us -> 30.8 us
    psum x2 -> x0, waiting for transfers between devices: 233 us -> none  [the longest x1 121 us: body(): spectrum_gram = lax.psum(local_spec, 'pix') / jnp.float32(PATCHES)]
    ppermute x0 -> x20, waiting for transfers between devices: none -> 85.3 us  [swap(): return lax.ppermute(x, 'pix', [(i, i ^ s) for i in range(n)])]
    unnamed x5 -> x0, waiting for transfers between devices: 85 us -> none
    all_gather x1 -> x0, waiting for transfers between devices: 64.7 us -> none  [body(): lax.all_gather(sketch, 'pix', axis=0, tiled=True)]
    ppermute x0 -> x20, starting transfers between devices: none -> 30.1 us  [swap(): return lax.ppermute(x, 'pix', [(i, i ^ s) for i in range(n)])]
    add x0 -> x13, other arithmetic: none -> 4.42 us  [the longest x4 4.34 us: scatter_sum(): b = keep + swap(send, s, n)]
    another operation x2 -> x11, other arithmetic: 10.5 us -> 14 us  [the longest x2 10.5 us: body(): jax.scipy.linalg.solve_triangular(lower, jnp.eye(lower.shape[0], dtype=jn...]
    dot_general x4 -> x8, matrix products: 10.3 us -> 7.83 us  [dot(): lax.dot_general(a, b, (contract, ((), ())), precision=precision, preferre...]
  transfers between devices with their start and end apart: 4 -> 20, of which waited for: 4 -> 17; matrix products, arithmetic and copies ran while one was open for 8% -> 16% of each run, Pallas kernels for 0% -> 0%
where the time goes in v1:
time: 163 us
  waiting for transfers between devices  85.3 us (52%)
  other arithmetic  30.8 us (19%)
  starting transfers between devices  30.1 us (18%)
  matrix products  8.07 us (5%)
  local copies, waits for them, and re-layouts  7.54 us (5%)
    ppermute x20, waiting for transfers between devices, swap(): return lax.ppermute(x, 'pix', [(i, i ^ s) for i in range(n)])  85.3 us
    ppermute x20, starting transfers between devices, swap(): return lax.ppermute(x, 'pix', [(i, i ^ s) for i in range(n)])  30.1 us
    another operation x3, other arithmetic, body(): lower = jnp.linalg.cholesky(gram)  12.4 us
    another operation x2, other arithmetic, body(): jax.scipy.linalg.solve_triangular(lower, jnp.eye(lower.shape[0], dtype=jn...  10.5 us
    dot_general x8, matrix products, dot(): lax.dot_general(a, b, (contract, ((), ())), precision=precision, preferre...  7.83 us
    add x4, other arithmetic, scatter_sum(): b = keep + swap(send, s, n)  4.34 us
    dot_general x1, local copies, waits for them, and re-layouts, dot(): lax.dot_general(a, b, (contract, ((), ())), precision=precision, preferre...  3.53 us
    another operation x9, other arithmetic, gather_rows(): b = jnp.stack([low, high], axis=1).reshape(-1, rows, cols)  3.52 us
  transfers between devices with their start and end apart: 20, of which 17 were waited for; matrix products, arithmetic and copies ran while one was open for 16% of the time, Pallas kernels for 0%

profile of v1, /device:TPU:0, one launch (start us, length us, event | category | flops | bytes accessed | tf_op | source)
XLA Modules:
  0.0 162.8 jit_solution(12520584836099297438)
XLA Ops:
  0.6 4.1 %collective-permute-start = (f32[1,192,128]{2,1,0:T(8,128)}, f32[1,192,128]{2,1,0:T(8,128)S(1)}, u32[]{:S(2)}, u32[]{:S(2)}) collective-permute-start(f32[1,192,128]{2,1,0:T(8,128)} %bitcast.101), channel_id=1, source_target_pairs={{0,16},{1,17},{2,18},{3,19},{4,20},{5,21},{6,22},{7,23},{8,24},{9,... | collective-permute-start | bytes 294920 | tf_op jit(solution)/shard_map/ppermute | solution.py:27
  4.8 5.1 %collective-permute-done = f32[1,192,128]{2,1,0:T(8,128)S(1)} collective-permute-done((f32[1,192,128]{2,1,0:T(8,128)}, f32[1,192,128]{2,1,0:T(8,128)S(1)}, u32[]{:S(2)}, u32[]{:S(2)}) %collective-permute-start) | collective-permute-done | bytes 98336 | tf_op jit(solution)/shard_map/ppermute | solution.py:27
  9.9 0.9 select_bitcast_fusion.9
  10.8 0.9 collective-permute-start.1
  11.7 5.2 %collective-permute-done.1 = f32[2,192,128]{2,1,0:T(8,128)S(1)} collective-permute-done((f32[2,192,128]{2,1,0:T(8,128)S(1)}, f32[2,192,128]{2,1,0:T(8,128)S(1)}, u32[]{:S(2)}, u32[]{:S(2)}) %collective-permute-start.1) | collective-permute-done | bytes 196640 | tf_op jit(solution)/shard_map/ppermute | solution.py:27
  17.0 1.4 collective-permute-start.2
  18.5 8.1 %collective-permute-done.2 = f32[4,192,128]{2,1,0:T(8,128)S(1)} collective-permute-done((f32[4,192,128]{2,1,0:T(8,128)S(1)}, f32[4,192,128]{2,1,0:T(8,128)S(1)}, u32[]{:S(2)}, u32[]{:S(2)}) %collective-permute-start.2) | collective-permute-done | bytes 393248 | tf_op jit(solution)/shard_map/ppermute | solution.py:27
  26.7 1.4 collective-permute-start.3
  28.1 15.6 %collective-permute-done.3 = f32[8,192,128]{2,1,0:T(8,128)S(1)} collective-permute-done((f32[8,192,128]{2,1,0:T(8,128)S(1)}, f32[8,192,128]{2,1,0:T(8,128)S(1)}, u32[]{:S(2)}, u32[]{:S(2)}) %collective-permute-start.3) | collective-permute-done | bytes 786464 | tf_op jit(solution)/shard_map/ppermute | solution.py:27
  44.3 3.5 %collective-permute-done.4 = f32[16,192,128]{2,1,0:T(8,128)} collective-permute-done((f32[16,192,128]{2,1,0:T(8,128)S(1)}, f32[16,192,128]{2,1,0:T(8,128)}, u32[]{:S(2)}, u32[]{:S(2)}) %collective-permute-start.4) | collective-permute-done | bytes 1572896 | tf_op jit(solution)/shard_map/ppermute | solution.py:27
  47.8 1.8 %select_bitcast_fusion.1 = (f32[16,1,192,128]{3,2,0,1:T(8,128)S(1)}, f32[16,1,192,128]{3,2,0,1:T(8,128)S(1)}) fusion(f32[16,192,128]{2,1,0:T(8,128)} %collective-permute-done.4, pred[]{:T(512)S(6)} %eq.32, f32[8,2,192,128]{3,2,1,0:T(8,128)S(1)} %copy.26), kind=kLoop, calls=%fused_computation.6 | loop fusion | flops 786432 | bytes 6291457 | tf_op jit(solution)/shard_map/stack | solution.py:38
  50.3 1.1 fusion.12
  51.5 3.1 %convolution_bitcast_fusion = f32[6144,128]{0,1:T(8,128)} fusion(f32[128,64]{0,1:T(8,128)S(1)} %fusion.12, f32[64,6144]{1,0:T(8,128)S(1)} %copy-done), kind=kOutput, calls=%fused_computation | convolution fusion | flops 301989888 | bytes 4751360 | tf_op jit(solution)/shard_map/dot_general | solution.py:11
  54.6 3.5 %copy.31 = f32[6144,128]{1,0:T(8,128)} copy(f32[6144,128]{0,1:T(8,128)} %convolution_bitcast_fusion) | data formatting | bytes 6291456 | tf_op jit(solution)/shard_map/dot_general | solution.py:11
  58.1 1.5 dynamic-slice_bitcast_fusion
  59.8 3.4 %collective-permute-done.10 = f32[16,192,128]{2,1,0:T(8,128)} collective-permute-done((f32[16,192,128]{2,1,0:T(8,128)S(1)}, f32[16,192,128]{2,1,0:T(8,128)}, u32[]{:S(2)}, u32[]{:S(2)}) %collective-permute-start.10) | collective-permute-done | bytes 1572896 | tf_op jit(solution)/shard_map/ppermute | solution.py:27
  63.2 2.0 %bitcast_add_fusion = f32[16,192,128]{2,1,0:T(8,128)S(1)} fusion(f32[16,192,128]{2,1,0:T(8,128)} %collective-permute-done.10, f32[16,2,192,128]{3,2,1,0:T(8,128)} %bitcast.90, s32[]{:T(128)S(6)} %select_n.176), kind=kLoop, calls=%fused_computation.3 | loop fusion | flops 393216 | bytes 4718596 | tf_op jit(solution)/shard_map/add | solution.py:50
  65.3 0.9 dynamic-slice_bitcast_fusion.1
  66.2 1.4 collective-permute-start.11
  67.6 18.5 %collective-permute-done.11 = f32[8,192,128]{2,1,0:T(8,128)} collective-permute-done((f32[8,192,128]{2,1,0:T(8,128)}, f32[8,192,128]{2,1,0:T(8,128)}, u32[]{:S(2)}, u32[]{:S(2)}) %collective-permute-start.11) | collective-permute-done | bytes 786464 | tf_op jit(solution)/shard_map/ppermute | solution.py:27
  86.1 1.2 bitcast_add_fusion.1
  87.4 0.9 copy-done.1
  88.3 1.5 collective-permute-start.12
  90.1 1.2 collective-permute-done.5
  91.3 1.6 collective-permute-start.6
  92.9 2.8 %collective-permute-done.6 = f32[128,128]{0,1:T(8,128)S(1)} collective-permute-done((f32[128,128]{0,1:T(8,128)S(1)}, f32[128,128]{0,1:T(8,128)S(1)}, u32[]{:S(2)}, u32[]{:S(2)}) %collective-permute-start.6) | collective-permute-done | bytes 65568 | tf_op jit(solution)/shard_map/ppermute | solution.py:27
  95.7 0.7 collective-permute-start.7
  96.4 3.6 %collective-permute-done.7 = f32[128,128]{0,1:T(8,128)S(1)} collective-permute-done((f32[128,128]{0,1:T(8,128)S(1)}, f32[128,128]{0,1:T(8,128)S(1)}, u32[]{:S(2)}, u32[]{:S(2)}) %collective-permute-start.7) | collective-permute-done | bytes 65568 | tf_op jit(solution)/shard_map/ppermute | solution.py:27
  100.0 3.3 %collective-permute-start.8 = (f32[128,128]{0,1:T(8,128)S(1)}, f32[128,128]{0,1:T(8,128)S(1)}, u32[]{:S(2)}, u32[]{:S(2)}) collective-permute-start(f32[128,128]{0,1:T(8,128)S(1)} %add.130), channel_id=1, source_target_pairs={{0,8},{1,9},{2,10},{3,11},{4,12},{5,13},{6,14},{7,15},{8,0},{9,1},... | collective-permute-start | bytes 196616 | tf_op jit(solution)/shard_map/ppermute | solution.py:27
  103.3 2.2 %collective-permute-done.8 = f32[128,128]{0,1:T(8,128)S(1)} collective-permute-done((f32[128,128]{0,1:T(8,128)S(1)}, f32[128,128]{0,1:T(8,128)S(1)}, u32[]{:S(2)}, u32[]{:S(2)}) %collective-permute-start.8) | collective-permute-done | bytes 65568 | tf_op jit(solution)/shard_map/ppermute | solution.py:27
  105.6 4.2 %collective-permute-start.9 = (f32[128,128]{0,1:T(8,128)S(1)}, f32[128,128]{0,1:T(8,128)S(1)}, u32[]{:S(2)}, u32[]{:S(2)}) collective-permute-start(f32[128,128]{0,1:T(8,128)S(1)} %add.131), channel_id=1, source_target_pairs={{0,16},{1,17},{2,18},{3,19},{4,20},{5,21},{6,22},{7,23},{8,24},{9,... | collective-permute-start | bytes 196616 | tf_op jit(solution)/shard_map/ppermute | solution.py:27
  109.8 2.3 %collective-permute-done.9 = f32[128,128]{0,1:T(8,128)S(1)} collective-permute-done((f32[128,128]{0,1:T(8,128)S(1)}, f32[128,128]{0,1:T(8,128)S(1)}, u32[]{:S(2)}, u32[]{:S(2)}) %collective-permute-start.9) | collective-permute-done | bytes 65568 | tf_op jit(solution)/shard_map/ppermute | solution.py:27
  112.1 1.0 bitcast_add_fusion.2
  113.2 1.5 collective-permute-start.13
  114.7 11.7 %cholesky.17 = f32[128,128]{1,0:T(8,128)S(1)} custom-call(f32[128,128]{1,0:T(8,128)S(1)} %fusion.7), custom_call_target="Cholesky" | custom-call | tf_op jit(solution)/shard_map/jit(cholesky)/cholesky | solution.py:69
  126.5 3.4 %collective-permute-start.14 = (f32[1,192,128]{2,1,0:T(8,128)S(1)}, f32[1,192,128]{2,1,0:T(8,128)S(1)}, u32[]{:S(2)}, u32[]{:S(2)}) collective-permute-start(f32[1,192,128]{2,1,0:T(8,128)S(1)} %constant_dynamic-slice_fusion), channel_id=1, source_target_pairs={{0,16},{1,17},{2,18},{3,19},{4,20},{5,21},{6,22},{7,23},{8,24},{9,... | collective-permute-start | bytes 294920 | tf_op jit(solution)/shard_map/ppermute | solution.py:27
  130.0 3.3 %collective-permute-done.14 = f32[1,192,128]{2,1,0:T(8,128)S(1)} collective-permute-done((f32[1,192,128]{2,1,0:T(8,128)S(1)}, f32[1,192,128]{2,1,0:T(8,128)S(1)}, u32[]{:S(2)}, u32[]{:S(2)}) %collective-permute-start.14) | collective-permute-done | bytes 98336 | tf_op jit(solution)/shard_map/ppermute | solution.py:27
  133.8 0.6 compare_reduce_fusion
  135.0 1.6 collective-permute-start.16
  136.6 0.7 fusion.4
  137.3 9.8 %custom-call.7 = f32[1,128,128]{1,2,0:T(8,128)S(1)} custom-call(f32[1,128,128]{2,1,0:T(8,128)S(1)} %fusion.4), custom_call_target="InvertDiagBlocksLowerTriangular" | custom-call | tf_op jit(solution)/shard_map/jit(_solve_triangular)/triangular_solve | solution.py:70
  147.6 3.8 %collective-permute-done.17 = f32[128,128]{1,0:T(8,128)S(1)} collective-permute-done((f32[128,128]{1,0:T(8,128)S(1)}, f32[128,128]{1,0:T(8,128)S(1)}, u32[]{:S(2)}, u32[]{:S(2)}) %collective-permute-start.17) | collective-permute-done | bytes 65568 | tf_op jit(solution)/shard_map/ppermute | solution.py:27
  151.7 0.9 convolution_multiply_fusion.1
  152.6 3.2 %collective-permute-done.18 = f32[128,128]{1,0:T(8,128)S(1)} collective-permute-done((f32[128,128]{1,0:T(8,128)S(1)}, f32[128,128]{1,0:T(8,128)S(1)}, u32[]{:S(2)}, u32[]{:S(2)}) %collective-permute-start.18) | collective-permute-done | bytes 65568 | tf_op jit(solution)/shard_map/ppermute | solution.py:27
  155.8 2.3 %collective-permute-start.19 = (f32[128,128]{1,0:T(8,128)S(1)}, f32[128,128]{1,0:T(8,128)S(1)}, u32[]{:S(2)}, u32[]{:S(2)}) collective-permute-start(f32[128,128]{1,0:T(8,128)S(1)} %add.152), channel_id=1, source_target_pairs={{0,16},{1,17},{2,18},{3,19},{4,20},{5,21},{6,22},{7,23},{8,24},{9,... | collective-permute-start | bytes 196616 | tf_op jit(solution)/shard_map/ppermute | solution.py:27
  158.1 0.9 fusion.2
  159.0 2.7 %collective-permute-done.19 = f32[128,128]{1,0:T(8,128)S(1)} collective-permute-done((f32[128,128]{1,0:T(8,128)S(1)}, f32[128,128]{1,0:T(8,128)S(1)}, u32[]{:S(2)}, u32[]{:S(2)}) %collective-permute-start.19) | collective-permute-done | bytes 65568 | tf_op jit(solution)/shard_map/ppermute | solution.py:27
  161.9 0.9 convolution_multiply_fusion
  (44 shorter events, 4.4 us)
Async XLA Ops:
  0.6 49.7 %copy-start = (f32[64,6144]{1,0:T(8,128)S(1)}, f32[64,6144]{1,0:T(8,128)}, u32[]{:S(2)}) copy-start(f32[64,6144]{1,0:T(8,128)} %param.2) | copy-start | bytes 4718596
  0.6 9.2 %collective-permute-start = (f32[1,192,128]{2,1,0:T(8,128)}, f32[1,192,128]{2,1,0:T(8,128)S(1)}, u32[]{:S(2)}, u32[]{:S(2)}) collective-permute-start(f32[1,192,128]{2,1,0:T(8,128)} %bitcast.101), channel_id=1, source_target_pairs={{0,16},{1,17},{2,18},{3,19},{4,20},{5,21},{6,22},{7,23},{8,24},{9,... | collective-permute-start | bytes 294920 | tf_op jit(solution)/shard_map/ppermute | solution.py:27
  10.8 6.1 %collective-permute-start.1 = (f32[2,192,128]{2,1,0:T(8,128)S(1)}, f32[2,192,128]{2,1,0:T(8,128)S(1)}, u32[]{:S(2)}, u32[]{:S(2)}) collective-permute-start(f32[2,192,128]{2,1,0:T(8,128)S(1)} %maximum_bitcast_fusion), channel_id=1, source_target_pairs={{0,8},{1,9},{2,10},{3,11},{4,12},{5,13},{6,14},{7,15},{8,0},{9,1},... | collective-permute-start | bytes 589832 | tf_op jit(solution)/shard_map/ppermute | solution.py:27
  17.0 9.5 %collective-permute-start.2 = (f32[4,192,128]{2,1,0:T(8,128)S(1)}, f32[4,192,128]{2,1,0:T(8,128)S(1)}, u32[]{:S(2)}, u32[]{:S(2)}) collective-permute-start(f32[4,192,128]{2,1,0:T(8,128)S(1)} %bitcast.98), channel_id=1, source_target_pairs={{0,4},{1,5},{2,6},{3,7},{4,0},{5,1},{6,2},{7,3},{8,12},{9,13},{10,... | collective-permute-start | bytes 1179656 | tf_op jit(solution)/shard_map/ppermute | solution.py:27
  26.7 17.1 %collective-permute-start.3 = (f32[8,192,128]{2,1,0:T(8,128)S(1)}, f32[8,192,128]{2,1,0:T(8,128)S(1)}, u32[]{:S(2)}, u32[]{:S(2)}) collective-permute-start(f32[8,192,128]{2,1,0:T(8,128)S(1)} %bitcast.97), channel_id=1, source_target_pairs={{0,2},{1,3},{2,0},{3,1},{4,6},{5,7},{6,4},{7,5},{8,10},{9,11},{10,... | collective-permute-start | bytes 2359304 | tf_op jit(solution)/shard_map/ppermute | solution.py:27
  44.2 3.6 %collective-permute-start.4 = (f32[16,192,128]{2,1,0:T(8,128)S(1)}, f32[16,192,128]{2,1,0:T(8,128)}, u32[]{:S(2)}, u32[]{:S(2)}) collective-permute-start(f32[16,192,128]{2,1,0:T(8,128)S(1)} %bitcast.94), channel_id=1, source_target_pairs={{0,1},{1,0},{2,3},{3,2},{4,5},{5,4},{6,7},{7,6},{8,9},{9,8},{10,11... | collective-permute-start | bytes 4718600 | tf_op jit(solution)/shard_map/ppermute | solution.py:27
  59.6 3.6 %collective-permute-start.10 = (f32[16,192,128]{2,1,0:T(8,128)S(1)}, f32[16,192,128]{2,1,0:T(8,128)}, u32[]{:S(2)}, u32[]{:S(2)}) collective-permute-start(f32[16,192,128]{2,1,0:T(8,128)S(1)} %dynamic-slice_bitcast_fusion), channel_id=1, source_target_pairs={{0,1},{1,0},{2,3},{3,2},{4,5},{5,4},{6,7},{7,6},{8,9},{9,8},{10,11... | collective-permute-start | bytes 4718600 | tf_op jit(solution)/shard_map/ppermute | solution.py:27
  66.2 19.9 %collective-permute-start.11 = (f32[8,192,128]{2,1,0:T(8,128)}, f32[8,192,128]{2,1,0:T(8,128)}, u32[]{:S(2)}, u32[]{:S(2)}) collective-permute-start(f32[8,192,128]{2,1,0:T(8,128)} %dynamic-slice_bitcast_fusion.1), channel_id=1, source_target_pairs={{0,2},{1,3},{2,0},{3,1},{4,6},{5,7},{6,4},{7,5},{8,10},{9,11},{10,... | collective-permute-start | bytes 2359304 | tf_op jit(solution)/shard_map/ppermute | solution.py:27
  87.3 0.9 copy-start.1
  88.3 23.9 %collective-permute-start.12 = (f32[4,192,128]{2,1,0:T(8,128)S(1)}, f32[4,192,128]{2,1,0:T(8,128)S(1)}, u32[]{:S(2)}, u32[]{:S(2)}) collective-permute-start(f32[4,192,128]{2,1,0:T(8,128)S(1)} %dynamic-slice_bitcast_fusion.2), channel_id=1, source_target_pairs={{0,4},{1,5},{2,6},{3,7},{4,0},{5,1},{6,2},{7,3},{8,12},{9,13},{10,... | collective-permute-start | bytes 1179656 | tf_op jit(solution)/shard_map/ppermute | solution.py:27
  90.0 1.3 collective-permute-start.5
  91.3 4.3 %collective-permute-start.6 = (f32[128,128]{0,1:T(8,128)S(1)}, f32[128,128]{0,1:T(8,128)S(1)}, u32[]{:S(2)}, u32[]{:S(2)}) collective-permute-start(f32[128,128]{0,1:T(8,128)S(1)} %add.128), channel_id=1, source_target_pairs={{0,2},{1,3},{2,0},{3,1},{4,6},{5,7},{6,4},{7,5},{8,10},{9,11},{10,... | collective-permute-start | bytes 196616 | tf_op jit(solution)/shard_map/ppermute | solution.py:27
  95.7 4.3 %collective-permute-start.7 = (f32[128,128]{0,1:T(8,128)S(1)}, f32[128,128]{0,1:T(8,128)S(1)}, u32[]{:S(2)}, u32[]{:S(2)}) collective-permute-start(f32[128,128]{0,1:T(8,128)S(1)} %add.129), channel_id=1, source_target_pairs={{0,4},{1,5},{2,6},{3,7},{4,0},{5,1},{6,2},{7,3},{8,12},{9,13},{10,... | collective-permute-start | bytes 196616 | tf_op jit(solution)/shard_map/ppermute | solution.py:27
  100.0 5.5 %collective-permute-start.8 = (f32[128,128]{0,1:T(8,128)S(1)}, f32[128,128]{0,1:T(8,128)S(1)}, u32[]{:S(2)}, u32[]{:S(2)}) collective-permute-start(f32[128,128]{0,1:T(8,128)S(1)} %add.130), channel_id=1, source_target_pairs={{0,8},{1,9},{2,10},{3,11},{4,12},{5,13},{6,14},{7,15},{8,0},{9,1},... | collective-permute-start | bytes 196616 | tf_op jit(solution)/shard_map/ppermute | solution.py:27
  105.6 6.4 %collective-permute-start.9 = (f32[128,128]{0,1:T(8,128)S(1)}, f32[128,128]{0,1:T(8,128)S(1)}, u32[]{:S(2)}, u32[]{:S(2)}) collective-permute-start(f32[128,128]{0,1:T(8,128)S(1)} %add.131), channel_id=1, source_target_pairs={{0,16},{1,17},{2,18},{3,19},{4,20},{5,21},{6,22},{7,23},{8,24},{9,... | collective-permute-start | bytes 196616 | tf_op jit(solution)/shard_map/ppermute | solution.py:27
  113.2 13.2 %collective-permute-start.13 = (f32[2,192,128]{2,1,0:T(8,128)S(1)}, f32[2,192,128]{2,1,0:T(8,128)S(1)}, u32[]{:S(2)}, u32[]{:S(2)}) collective-permute-start(f32[2,192,128]{2,1,0:T(8,128)S(1)} %dynamic-slice_bitcast_fusion.3), channel_id=1, source_target_pairs={{0,8},{1,9},{2,10},{3,11},{4,12},{5,13},{6,14},{7,15},{8,0},{9,1},... | collective-permute-start | bytes 589832 | tf_op jit(solution)/shard_map/ppermute | solution.py:27
  126.5 6.7 %collective-permute-start.14 = (f32[1,192,128]{2,1,0:T(8,128)S(1)}, f32[1,192,128]{2,1,0:T(8,128)S(1)}, u32[]{:S(2)}, u32[]{:S(2)}) collective-permute-start(f32[1,192,128]{2,1,0:T(8,128)S(1)} %constant_dynamic-slice_fusion), channel_id=1, source_target_pairs={{0,16},{1,17},{2,18},{3,19},{4,20},{5,21},{6,22},{7,23},{8,24},{9,... | collective-permute-start | bytes 294920 | tf_op jit(solution)/shard_map/ppermute | solution.py:27
  133.7 1.3 collective-permute-start.15
  135.0 12.0 %collective-permute-start.16 = (f32[128,128]{1,0:T(8,128)S(1)}, f32[128,128]{1,0:T(8,128)S(1)}, u32[]{:S(2)}, u32[]{:S(2)}) collective-permute-start(f32[128,128]{1,0:T(8,128)S(1)} %add.149), channel_id=1, source_target_pairs={{0,2},{1,3},{2,0},{3,1},{4,6},{5,7},{6,4},{7,5},{8,10},{9,11},{10,... | collective-permute-start | bytes 196616 | tf_op jit(solution)/shard_map/ppermute | solution.py:27
  147.1 4.3 %collective-permute-start.17 = (f32[128,128]{1,0:T(8,128)S(1)}, f32[128,128]{1,0:T(8,128)S(1)}, u32[]{:S(2)}, u32[]{:S(2)}) collective-permute-start(f32[128,128]{1,0:T(8,128)S(1)} %add.150), channel_id=1, source_target_pairs={{0,4},{1,5},{2,6},{3,7},{4,0},{5,1},{6,2},{7,3},{8,12},{9,13},{10,... | collective-permute-start | bytes 196616 | tf_op jit(solution)/shard_map/ppermute | solution.py:27
  151.5 4.3 %collective-permute-start.18 = (f32[128,128]{1,0:T(8,128)S(1)}, f32[128,128]{1,0:T(8,128)S(1)}, u32[]{:S(2)}, u32[]{:S(2)}) collective-permute-start(f32[128,128]{1,0:T(8,128)S(1)} %add.151), channel_id=1, source_target_pairs={{0,8},{1,9},{2,10},{3,11},{4,12},{5,13},{6,14},{7,15},{8,0},{9,1},... | collective-permute-start | bytes 196616 | tf_op jit(solution)/shard_map/ppermute | solution.py:27
  155.8 5.8 %collective-permute-start.19 = (f32[128,128]{1,0:T(8,128)S(1)}, f32[128,128]{1,0:T(8,128)S(1)}, u32[]{:S(2)}, u32[]{:S(2)}) collective-permute-start(f32[128,128]{1,0:T(8,128)S(1)} %add.152), channel_id=1, source_target_pairs={{0,16},{1,17},{2,18},{3,19},{4,20},{5,21},{6,22},{7,23},{8,24},{9,... | collective-permute-start | bytes 196616 | tf_op jit(solution)/shard_map/ppermute | solution.py:27

commit v2 on v1

v2 whole, which is shorter than its diff:
```python
import jax
import jax.numpy as jnp
from jax import lax
from jax.sharding import PartitionSpec as P

HIGHEST = lax.Precision.HIGHEST
HIGH = lax.Precision.HIGH


def dot(a, b, contract, precision=HIGHEST):
    return lax.dot_general(
        a, b, (contract, ((), ())), precision=precision, preferred_element_type=jnp.float32
    )


def swap(x, s, n):
    return lax.ppermute(x, "pix", [(i, i ^ s) for i in range(n)])


def body(green, sketch):
    n = lax.axis_size("pix")
    assert n & (n - 1) == 0 and n >= 8
    me = lax.axis_index("pix")
    pixels, patches = green.shape
    rows, rank = sketch.shape
    top = n // 2
    middle = [1 << k for k in range(1, n.bit_length() - 2)]
    core = me % 2
    high = me // top
    own_half = core == high
    crossing = [(i, i ^ top ^ 1) for i in range(n) if i % 2 != i // top]

    def bit(s):
        return (me // s) % 2

    def cross(x):
        return lax.ppermute(x, "pix", crossing)

    def gather(b, order):
        done = []
        for s in order:
            other = swap(b, s, n)
            axis = sum(d > s for d in done)
            b = jnp.stack(
                [jnp.where(bit(s) == 0, b, other), jnp.where(bit(s) == 0, other, b)], axis=axis
            )
            done.append(s)
        return b

    def scatter(b, order):
        left = sorted(order, reverse=True)
        for s in order:
            axis = left.index(s)
            keep = lax.dynamic_index_in_dim(b, bit(s), axis, False)
            send = lax.dynamic_index_in_dim(b, 1 - bit(s), axis, False)
            b = keep + swap(send, s, n)
            left.remove(s)
        return b

    def total(x, order):
        for s in order:
            x = x + swap(x, s, n)
        return x

    tail = middle[2:][::-1]
    order_a = tail + middle[:2][::-1]
    order_b = tail + middle[:2]

    other = swap(sketch, 1, n)
    pair = jnp.stack([jnp.where(core == 0, sketch, other), jnp.where(core == 0, other, sketch)])
    pair = jnp.where(own_half, pair, cross(pair))
    halves = [gather(pair[0], order_a), gather(pair[1], order_b)]
    block = jnp.stack(halves, axis=-3).reshape(patches // 2, rank)

    half = patches // 2
    first, second = green[:, :half], green[:, half:]
    keep = jnp.where(core == 0, first, second)
    took = swap(jnp.where(core == 0, second, first), 1, n)
    both = jnp.concatenate(
        [jnp.where(core == 0, keep, took), jnp.where(core == 0, took, keep)], axis=0
    )

    part = dot(both, block, ((1,), (0,)), HIGH)
    sketched = part + swap(part, 1, n)
    gram = total(dot(sketched, sketched, ((0,), (0,))), [top] + middle[::-1])

    partial = dot(both, sketched, ((0,), (0,)), HIGH)
    partial = partial.reshape([2] * len(middle) + [2, rows, rank])
    sums = jnp.stack(
        [
            scatter(partial[..., 0, :, :], order_a[::-1]),
            scatter(partial[..., 1, :, :], order_b[::-1]),
        ]
    )
    sums = jnp.where(own_half, sums, cross(sums))
    raw = lax.dynamic_index_in_dim(sums, core, 0, False) + swap(
        lax.dynamic_index_in_dim(sums, 1 - core, 0, False), 1, n
    )
    raw_gram = total(dot(raw, raw, ((0,), (0,))), [1] + middle + [top])

    lower = jnp.linalg.cholesky(gram)
    inverse = jax.scipy.linalg.solve_triangular(lower, jnp.eye(rank, dtype=jnp.float32), lower=True)
    mine = lax.dynamic_slice_in_dim(sketched, core * pixels, pixels, 0)
    basis = jnp.sqrt(jnp.float32(pixels * n)) * dot(mine, inverse, ((1,), (1,)))
    projection = dot(raw, inverse, ((1,), (1,)))
    spectrum = dot(dot(inverse, raw_gram, ((1,), (0,))), inverse, ((1,), (1,)))
    return (basis, projection, spectrum / jnp.float32(patches))


def solution(mesh):
    in_specs = (P("pix", None), P("pix", None))
    out_specs = (P("pix", None), P("pix", None), P())

    return jax.shard_map(body, mesh=mesh, in_specs=in_specs, out_specs=out_specs, check_vma=False)
```

time: 163 us -> 130 us (0.80)
  waiting for transfers between devices: 85.3 us -> 61 us
  local copies, waits for them, and re-layouts: 7.54 us -> 0.4 us
  other arithmetic: 30.8 us -> 25.9 us
  starting transfers between devices: 30.1 us -> 34.7 us
  matrix products: 8.07 us -> 6.25 us
    ppermute x20 -> x25, waiting for transfers between devices: 85.3 us -> 61 us  [swap(): return lax.ppermute(x, 'pix', [(i, i ^ s) for i in range(n)])]
    add x4 -> x5, other arithmetic: 4.34 us -> 0.15 us  [the longest x4 0.14 us: scatter(): b = keep + swap(send, s, n)]
    dot_general x1 -> x0, local copies, waits for them, and re-layouts: 3.53 us -> none  [dot(): lax.dot_general(a, b, (contract, ((), ())), precision=precision, preferre...]
    ppermute x20 -> x25, starting transfers between devices: 30.1 us -> 33.2 us  [swap(): return lax.ppermute(x, 'pix', [(i, i ^ s) for i in range(n)])]
    squeeze x5 -> x8, local copies, waits for them, and re-layouts: 2.52 us -> 0.17 us  [the longest x6 0.14 us: scatter(): send = lax.dynamic_index_in_dim(b, 1 - bit(s), axis, False)]
    another operation x11 -> x18, other arithmetic: 14 us -> 11.9 us  [the longest x2 10.5 us: body(): jax.scipy.linalg.solve_triangular(lower, jnp.eye(rank, dtype=jnp.float32)...]
    dot_general x8, matrix products: 7.83 us -> 6 us  [dot(): lax.dot_general(a, b, (contract, ((), ())), precision=precision, preferre...]
  transfers between devices with their start and end apart: 20 -> 27, of which waited for: 17 -> 20; matrix products, arithmetic and copies ran while one was open for 16% -> 21% of each run, Pallas kernels for 0% -> 0%
where the time goes in v2:
time: 130 us; the launch traced here: 129 us
  waiting for transfers between devices  61 us (47%)
  starting transfers between devices  34.7 us (27%)
  other arithmetic  25.9 us (20%)
  matrix products  6.25 us (5%)
    ppermute x25, waiting for transfers between devices, swap(): return lax.ppermute(x, 'pix', [(i, i ^ s) for i in range(n)])  61 us
    ppermute x25, starting transfers between devices, swap(): return lax.ppermute(x, 'pix', [(i, i ^ s) for i in range(n)])  33.2 us
    another operation x3, other arithmetic, body(): lower = jnp.linalg.cholesky(gram)  12.4 us
    another operation x2, other arithmetic, body(): jax.scipy.linalg.solve_triangular(lower, jnp.eye(rank, dtype=jnp.float32)...  10.5 us
    dot_general x8, matrix products, dot(): lax.dot_general(a, b, (contract, ((), ())), precision=precision, preferre...  6 us
  transfers between devices with their start and end apart: 27, of which 20 were waited for; matrix products, arithmetic and copies ran while one was open for 21% of the time, Pallas kernels for 0%

profile of v2, /device:TPU:0, one launch (start us, length us, event | category | flops | bytes accessed | tf_op | source)
XLA Modules:
  0.0 129.4 jit_solution(17721634529498392344)
XLA Ops:
  0.6 0.6 collective-permute-start.1
  1.2 1.2 collective-permute-done.1
  2.4 0.9 select_bitcast_fusion.13
  3.3 0.7 collective-permute-start.2
  4.1 3.0 %collective-permute-start.3 = (f32[192,128]{1,0:T(8,128)S(1)}, f32[192,128]{1,0:T(8,128)S(1)}, u32[]{:S(2)}, u32[]{:S(2)}) collective-permute-start(f32[192,128]{1,0:T(8,128)S(1)} %get-tuple-element.21), channel_id=1, source_target_pairs={{0,8},{1,9},{2,10},{3,11},{4,12},{5,13},{6,14},{7,15},{8,0},{9,1},... | collective-permute-start | bytes 294920 | tf_op jit(solution)/shard_map/ppermute | solution.py:17
  7.1 2.5 %collective-permute-done.3 = f32[192,128]{1,0:T(8,128)S(1)} collective-permute-done((f32[192,128]{1,0:T(8,128)S(1)}, f32[192,128]{1,0:T(8,128)S(1)}, u32[]{:S(2)}, u32[]{:S(2)}) %collective-permute-start.3) | collective-permute-done | bytes 98336 | tf_op jit(solution)/shard_map/ppermute | solution.py:17
  9.6 4.0 %collective-permute-done.6 = f32[192,128]{1,0:T(8,128)S(1)} collective-permute-done((f32[192,128]{1,0:T(8,128)S(1)}, f32[192,128]{1,0:T(8,128)S(1)}, u32[]{:S(2)}, u32[]{:S(2)}) %collective-permute-start.6) | collective-permute-done | bytes 98336 | tf_op jit(solution)/shard_map/ppermute | solution.py:17
  13.7 1.5 %collective-permute-start.4 = (f32[2,192,128]{2,1,0:T(8,128)S(1)}, f32[2,192,128]{2,1,0:T(8,128)S(1)}, u32[]{:S(2)}, u32[]{:S(2)}) collective-permute-start(f32[2,192,128]{2,1,0:T(8,128)S(1)} %pad_maximum_fusion.7), channel_id=1, source_target_pairs={{0,4},{1,5},{2,6},{3,7},{4,0},{5,1},{6,2},{7,3},{8,12},{9,13},{10,... | collective-permute-start | bytes 589832 | tf_op jit(solution)/shard_map/ppermute | solution.py:17
  15.3 5.7 %collective-permute-start = (f32[64,3072]{1,0:T(8,128)S(1)}, f32[64,3072]{1,0:T(8,128)}, u32[]{:S(2)}, u32[]{:S(2)}) collective-permute-start(f32[64,3072]{1,0:T(8,128)S(1)} %slice_select_fusion), channel_id=1, source_target_pairs={{0,1},{1,0},{2,3},{3,2},{4,5},{5,4},{6,7},{7,6},{8,9},{9,8},{10,11... | collective-permute-start | bytes 2359304 | tf_op jit(solution)/shard_map/ppermute | solution.py:17
  21.0 1.6 %collective-permute-start.7 = (f32[2,192,128]{2,1,0:T(8,128)S(1)}, f32[2,192,128]{2,1,0:T(8,128)S(1)}, u32[]{:S(2)}, u32[]{:S(2)}) collective-permute-start(f32[2,192,128]{2,1,0:T(8,128)S(1)} %pad_maximum_fusion.8), channel_id=1, source_target_pairs={{0,2},{1,3},{2,0},{3,1},{4,6},{5,7},{6,4},{7,5},{8,10},{9,11},{10,... | collective-permute-start | bytes 589832 | tf_op jit(solution)/shard_map/ppermute | solution.py:17
  22.6 0.6 collective-permute-start.5
  23.2 5.6 %collective-permute-done.7 = f32[2,192,128]{2,1,0:T(8,128)S(1)} collective-permute-done((f32[2,192,128]{2,1,0:T(8,128)S(1)}, f32[2,192,128]{2,1,0:T(8,128)S(1)}, u32[]{:S(2)}, u32[]{:S(2)}) %collective-permute-start.7) | collective-permute-done | bytes 196640 | tf_op jit(solution)/shard_map/ppermute | solution.py:17
  29.0 1.3 broadcast_select_fusion.1
  30.3 8.0 %collective-permute-done.8 = f32[2,2,192,128]{3,2,1,0:T(8,128)S(1)} collective-permute-done((f32[2,2,192,128]{3,2,1,0:T(8,128)S(1)}, f32[2,2,192,128]{3,2,1,0:T(8,128)S(1)}, u32[]{:S(2)}, u32[]{:S(2)}) %collective-permute-start.8) | collective-permute-done | bytes 393248 | tf_op jit(solution)/shard_map/ppermute | solution.py:17
  38.6 1.0 fusion.1
  39.7 1.2 collective-permute-done.9
  41.0 1.4 %fusion = f32[3072,128]{1,0:T(8,128)S(1)} fusion(f32[128,128]{1,0:T(8,128)S(1)} %add.146, f32[64,3072]{1,0:T(8,128)S(1)} %get-tuple-element.4, f32[64,3072]{1,0:T(8,128)S(1)} %get-tuple-element.3), kind=kOutput, calls=%fused_computation.2 | convolution fusion | flops 302383104 | bytes 3211264 | tf_op jit(solution)/shard_map/dot_general | solution.py:11
  42.6 1.6 %collective-permute-start.14 = (f32[2,2,192,128]{3,2,1,0:T(8,128)S(1)}, f32[2,2,192,128]{3,2,1,0:T(8,128)S(1)}, u32[]{:S(2)}, u32[]{:S(2)}) collective-permute-start(f32[2,2,192,128]{3,2,1,0:T(8,128)S(1)} %dynamic-slice_bitcast_fusion.1), channel_id=1, source_target_pairs={{0,2},{1,3},{2,0},{3,1},{4,6},{5,7},{6,4},{7,5},{8,10},{9,11},{10,... | collective-permute-start | bytes 1179656 | tf_op jit(solution)/shard_map/ppermute | solution.py:17
  44.4 5.1 %collective-permute-start.10 = (f32[128,128]{0,1:T(8,128)S(1)}, f32[128,128]{0,1:T(8,128)S(1)}, u32[]{:S(2)}, u32[]{:S(2)}) collective-permute-start(f32[128,128]{0,1:T(8,128)S(1)} %fusion.19), channel_id=1, source_target_pairs={{0,16},{1,17},{2,18},{3,19},{4,20},{5,21},{6,22},{7,23},{8,24},{9,... | collective-permute-start | bytes 196616 | tf_op jit(solution)/shard_map/ppermute | solution.py:17
  49.6 3.5 %collective-permute-done.10 = f32[128,128]{0,1:T(8,128)S(1)} collective-permute-done((f32[128,128]{0,1:T(8,128)S(1)}, f32[128,128]{0,1:T(8,128)S(1)}, u32[]{:S(2)}, u32[]{:S(2)}) %collective-permute-start.10) | collective-permute-done | bytes 65568 | tf_op jit(solution)/shard_map/ppermute | solution.py:17
  53.5 3.9 %collective-permute-done.11 = f32[128,128]{0,1:T(8,128)S(1)} collective-permute-done((f32[128,128]{0,1:T(8,128)S(1)}, f32[128,128]{0,1:T(8,128)S(1)}, u32[]{:S(2)}, u32[]{:S(2)}) %collective-permute-start.11) | collective-permute-done | bytes 65568 | tf_op jit(solution)/shard_map/ppermute | solution.py:17
  57.5 0.6 collective-permute-start.12
  58.0 3.8 %collective-permute-done.12 = f32[128,128]{0,1:T(8,128)S(1)} collective-permute-done((f32[128,128]{0,1:T(8,128)S(1)}, f32[128,128]{0,1:T(8,128)S(1)}, u32[]{:S(2)}, u32[]{:S(2)}) %collective-permute-start.12) | collective-permute-done | bytes 65568 | tf_op jit(solution)/shard_map/ppermute | solution.py:17
  61.8 0.6 collective-permute-start.13
  62.4 0.6 collective-permute-start.17
  63.0 3.1 %collective-permute-done.13 = f32[128,128]{0,1:T(8,128)S(1)} collective-permute-done((f32[128,128]{0,1:T(8,128)S(1)}, f32[128,128]{0,1:T(8,128)S(1)}, u32[]{:S(2)}, u32[]{:S(2)}) %collective-permute-start.13) | collective-permute-done | bytes 65568 | tf_op jit(solution)/shard_map/ppermute | solution.py:17
  66.3 0.6 collective-permute-start.15
  66.9 5.7 %collective-permute-done.17 = f32[2,2,192,128]{3,2,1,0:T(8,128)S(1)} collective-permute-done((f32[2,2,192,128]{3,2,1,0:T(8,128)S(1)}, f32[2,2,192,128]{3,2,1,0:T(8,128)S(1)}, u32[]{:S(2)}, u32[]{:S(2)}) %collective-permute-start.17) | collective-permute-done | bytes 393248 | tf_op jit(solution)/shard_map/ppermute | solution.py:17
  72.7 1.6 %collective-permute-start.18 = (f32[2,192,128]{2,1,0:T(8,128)S(1)}, f32[2,192,128]{2,1,0:T(8,128)S(1)}, u32[]{:S(2)}, u32[]{:S(2)}) collective-permute-start(f32[2,192,128]{2,1,0:T(8,128)S(1)} %dynamic-slice_bitcast_fusion.2), channel_id=1, source_target_pairs={{0,2},{1,3},{2,0},{3,1},{4,6},{5,7},{6,4},{7,5},{8,10},{9,11},{10,... | collective-permute-start | bytes 589832 | tf_op jit(solution)/shard_map/ppermute | solution.py:17
  75.1 3.3 %collective-permute-done.18 = f32[2,192,128]{2,1,0:T(8,128)S(1)} collective-permute-done((f32[2,192,128]{2,1,0:T(8,128)S(1)}, f32[2,192,128]{2,1,0:T(8,128)S(1)}, u32[]{:S(2)}, u32[]{:S(2)}) %collective-permute-start.18) | collective-permute-done | bytes 196640 | tf_op jit(solution)/shard_map/ppermute | solution.py:17
  78.8 0.6 collective-permute-done.16
  79.4 3.7 %collective-permute-done.19 = f32[192,128]{1,0:T(8,128)S(1)} collective-permute-done((f32[192,128]{1,0:T(8,128)S(1)}, f32[192,128]{1,0:T(8,128)S(1)}, u32[]{:S(2)}, u32[]{:S(2)}) %collective-permute-start.19) | collective-permute-done | bytes 98336 | tf_op jit(solution)/shard_map/ppermute | solution.py:17
  83.2 0.9 collective-permute-start.20
  84.0 11.7 %cholesky.17 = f32[128,128]{1,0:T(8,128)S(1)} custom-call(f32[128,128]{1,0:T(8,128)S(1)} %fusion.7), custom_call_target="Cholesky" | custom-call | tf_op jit(solution)/shard_map/jit(cholesky)/cholesky | solution.py:101
  95.8 3.7 %collective-permute-start.21 = (f32[192,128]{1,0:T(8,128)S(1)}, f32[192,128]{1,0:T(8,128)S(1)}, u32[]{:S(2)}, u32[]{:S(2)}) collective-permute-start(f32[192,128]{1,0:T(8,128)S(1)} %dynamic-slice_bitcast_fusion.4), channel_id=1, source_target_pairs={{0,1},{1,0},{2,3},{3,2},{4,5},{5,4},{6,7},{7,6},{8,9},{9,8},{10,11... | collective-permute-start | bytes 294920 | tf_op jit(solution)/shard_map/ppermute | solution.py:17
  99.6 0.9 collective-permute-done.21
  101.4 0.6 compare_reduce_fusion
  102.3 1.6 %collective-permute-start.23 = (f32[128,128]{1,0:T(8,128)S(1)}, f32[128,128]{1,0:T(8,128)S(1)}, u32[]{:S(2)}, u32[]{:S(2)}) collective-permute-start(f32[128,128]{1,0:T(8,128)S(1)} %add.168), channel_id=1, source_target_pairs={{0,2},{1,3},{2,0},{3,1},{4,6},{5,7},{6,4},{7,5},{8,10},{9,11},{10,... | collective-permute-start | bytes 196616 | tf_op jit(solution)/shard_map/ppermute | solution.py:17
  103.8 0.7 fusion.4
  104.5 9.8 %custom-call.7 = f32[1,128,128]{1,2,0:T(8,128)S(1)} custom-call(f32[1,128,128]{2,1,0:T(8,128)S(1)} %fusion.4), custom_call_target="InvertDiagBlocksLowerTriangular" | custom-call | tf_op jit(solution)/shard_map/jit(_solve_triangular)/triangular_solve | solution.py:102
  114.4 0.6 collective-permute-start.24
  115.2 3.5 %collective-permute-done.24 = f32[128,128]{1,0:T(8,128)S(1)} collective-permute-done((f32[128,128]{1,0:T(8,128)S(1)}, f32[128,128]{1,0:T(8,128)S(1)}, u32[]{:S(2)}, u32[]{:S(2)}) %collective-permute-start.24) | collective-permute-done | bytes 65568 | tf_op jit(solution)/shard_map/ppermute | solution.py:17
  118.7 1.8 %collective-permute-start.25 = (f32[128,128]{1,0:T(8,128)S(1)}, f32[128,128]{1,0:T(8,128)S(1)}, u32[]{:S(2)}, u32[]{:S(2)}) collective-permute-start(f32[128,128]{1,0:T(8,128)S(1)} %add.170), channel_id=1, source_target_pairs={{0,8},{1,9},{2,10},{3,11},{4,12},{5,13},{6,14},{7,15},{8,0},{9,1},... | collective-permute-start | bytes 196616 | tf_op jit(solution)/shard_map/ppermute | solution.py:17
  120.5 0.9 convolution_multiply_fusion.1
  121.4 1.7 %collective-permute-done.25 = f32[128,128]{1,0:T(8,128)S(1)} collective-permute-done((f32[128,128]{1,0:T(8,128)S(1)}, f32[128,128]{1,0:T(8,128)S(1)}, u32[]{:S(2)}, u32[]{:S(2)}) %collective-permute-start.25) | collective-permute-done | bytes 65568 | tf_op jit(solution)/shard_map/ppermute | solution.py:17
  123.4 0.9 fusion.11
  124.3 4.0 %collective-permute-done.26 = f32[128,128]{1,0:T(8,128)S(1)} collective-permute-done((f32[128,128]{1,0:T(8,128)S(1)}, f32[128,128]{1,0:T(8,128)S(1)}, u32[]{:S(2)}, u32[]{:S(2)}) %collective-permute-start.26) | collective-permute-done | bytes 65568 | tf_op jit(solution)/shard_map/ppermute | solution.py:17
  128.5 0.9 convolution_multiply_fusion
  (66 shorter events, 5.3 us)
Async XLA Ops:
  0.6 14.6 %copy-start = (f32[64,6144]{1,0:T(8,128)S(1)}, f32[64,6144]{1,0:T(8,128)}, u32[]{:S(2)}) copy-start(f32[64,6144]{1,0:T(8,128)} %param.2) | copy-start | bytes 4718596
  0.6 1.7 %collective-permute-start.1 = (f32[192,128]{1,0:T(8,128)}, f32[192,128]{1,0:T(8,128)S(1)}, u32[]{:S(2)}, u32[]{:S(2)}) collective-permute-start(f32[192,128]{1,0:T(8,128)} %param.3), channel_id=1, source_target_pairs={{0,1},{1,0},{2,3},{3,2},{4,5},{5,4},{6,7},{7,6},{8,9},{9,8},{10,11... | collective-permute-start | bytes 294920 | tf_op jit(solution)/shard_map/ppermute | solution.py:17
  3.3 0.7 collective-permute-start.2
  4.1 5.6 %collective-permute-start.3 = (f32[192,128]{1,0:T(8,128)S(1)}, f32[192,128]{1,0:T(8,128)S(1)}, u32[]{:S(2)}, u32[]{:S(2)}) collective-permute-start(f32[192,128]{1,0:T(8,128)S(1)} %get-tuple-element.21), channel_id=1, source_target_pairs={{0,8},{1,9},{2,10},{3,11},{4,12},{5,13},{6,14},{7,15},{8,0},{9,1},... | collective-permute-start | bytes 294920 | tf_op jit(solution)/shard_map/ppermute | solution.py:17
  7.0 6.6 %collective-permute-start.6 = (f32[192,128]{1,0:T(8,128)S(1)}, f32[192,128]{1,0:T(8,128)S(1)}, u32[]{:S(2)}, u32[]{:S(2)}) collective-permute-start(f32[192,128]{1,0:T(8,128)S(1)} %get-tuple-element.22), channel_id=1, source_target_pairs={{0,8},{1,9},{2,10},{3,11},{4,12},{5,13},{6,14},{7,15},{8,0},{9,1},... | collective-permute-start | bytes 294920 | tf_op jit(solution)/shard_map/ppermute | solution.py:17
  13.7 8.9 %collective-permute-start.4 = (f32[2,192,128]{2,1,0:T(8,128)S(1)}, f32[2,192,128]{2,1,0:T(8,128)S(1)}, u32[]{:S(2)}, u32[]{:S(2)}) collective-permute-start(f32[2,192,128]{2,1,0:T(8,128)S(1)} %pad_maximum_fusion.7), channel_id=1, source_target_pairs={{0,4},{1,5},{2,6},{3,7},{4,0},{5,1},{6,2},{7,3},{8,12},{9,13},{10,... | collective-permute-start | bytes 589832 | tf_op jit(solution)/shard_map/ppermute | solution.py:17
  15.3 13.7 %collective-permute-start = (f32[64,3072]{1,0:T(8,128)S(1)}, f32[64,3072]{1,0:T(8,128)}, u32[]{:S(2)}, u32[]{:S(2)}) collective-permute-start(f32[64,3072]{1,0:T(8,128)S(1)} %slice_select_fusion), channel_id=1, source_target_pairs={{0,1},{1,0},{2,3},{3,2},{4,5},{5,4},{6,7},{7,6},{8,9},{9,8},{10,11... | collective-permute-start | bytes 2359304 | tf_op jit(solution)/shard_map/ppermute | solution.py:17
  21.0 7.8 %collective-permute-start.7 = (f32[2,192,128]{2,1,0:T(8,128)S(1)}, f32[2,192,128]{2,1,0:T(8,128)S(1)}, u32[]{:S(2)}, u32[]{:S(2)}) collective-permute-start(f32[2,192,128]{2,1,0:T(8,128)S(1)} %pad_maximum_fusion.8), channel_id=1, source_target_pairs={{0,2},{1,3},{2,0},{3,1},{4,6},{5,7},{6,4},{7,5},{8,10},{9,11},{10,... | collective-permute-start | bytes 589832 | tf_op jit(solution)/shard_map/ppermute | solution.py:17
  22.6 15.8 %collective-permute-start.5 = (f32[2,2,192,128]{3,2,0,1:T(8,128)S(1)}, f32[2,2,192,128]{3,2,0,1:T(8,128)S(1)}, u32[]{:S(2)}, u32[]{:S(2)}) collective-permute-start(f32[2,2,192,128]{3,2,0,1:T(8,128)S(1)} %pad_maximum_fusion.4), channel_id=1, source_target_pairs={{0,2},{1,3},{2,0},{3,1},{4,6},{5,7},{6,4},{7,5},{8,10},{9,11},{10,... | collective-permute-start | bytes 1179656 | tf_op jit(solution)/shard_map/ppermute | solution.py:17
  28.9 9.4 %collective-permute-start.8 = (f32[2,2,192,128]{3,2,1,0:T(8,128)S(1)}, f32[2,2,192,128]{3,2,1,0:T(8,128)S(1)}, u32[]{:S(2)}, u32[]{:S(2)}) collective-permute-start(f32[2,2,192,128]{3,2,1,0:T(8,128)S(1)} %pad_maximum_fusion.5), channel_id=1, source_target_pairs={{0,4},{1,5},{2,6},{3,7},{4,0},{5,1},{6,2},{7,3},{8,12},{9,13},{10,... | collective-permute-start | bytes 1179656 | tf_op jit(solution)/shard_map/ppermute | solution.py:17
  39.6 1.3 %collective-permute-start.9 = (f32[128,128]{1,0:T(8,128)S(1)}, f32[128,128]{1,0:T(8,128)S(1)}, u32[]{:S(2)}, u32[]{:S(2)}) collective-permute-start(f32[128,128]{1,0:T(8,128)S(1)} %fusion.1), channel_id=1, source_target_pairs={{0,1},{1,0},{2,3},{3,2},{4,5},{5,4},{6,7},{7,6},{8,9},{9,8},{10,11... | collective-permute-start | bytes 196616 | tf_op jit(solution)/shard_map/ppermute | solution.py:17
  42.6 23.7 %collective-permute-start.14 = (f32[2,2,192,128]{3,2,1,0:T(8,128)S(1)}, f32[2,2,192,128]{3,2,1,0:T(8,128)S(1)}, u32[]{:S(2)}, u32[]{:S(2)}) collective-permute-start(f32[2,2,192,128]{3,2,1,0:T(8,128)S(1)} %dynamic-slice_bitcast_fusion.1), channel_id=1, source_target_pairs={{0,2},{1,3},{2,0},{3,1},{4,6},{5,7},{6,4},{7,5},{8,10},{9,11},{10,... | collective-permute-start | bytes 1179656 | tf_op jit(solution)/shard_map/ppermute | solution.py:17
  44.4 8.7 %collective-permute-start.10 = (f32[128,128]{0,1:T(8,128)S(1)}, f32[128,128]{0,1:T(8,128)S(1)}, u32[]{:S(2)}, u32[]{:S(2)}) collective-permute-start(f32[128,128]{0,1:T(8,128)S(1)} %fusion.19), channel_id=1, source_target_pairs={{0,16},{1,17},{2,18},{3,19},{4,20},{5,21},{6,22},{7,23},{8,24},{9,... | collective-permute-start | bytes 196616 | tf_op jit(solution)/shard_map/ppermute | solution.py:17
  53.1 4.3 %collective-permute-start.11 = (f32[128,128]{0,1:T(8,128)S(1)}, f32[128,128]{0,1:T(8,128)S(1)}, u32[]{:S(2)}, u32[]{:S(2)}) collective-permute-start(f32[128,128]{0,1:T(8,128)S(1)} %add.148), channel_id=1, source_target_pairs={{0,8},{1,9},{2,10},{3,11},{4,12},{5,13},{6,14},{7,15},{8,0},{9,1},... | collective-permute-start | bytes 196616 | tf_op jit(solution)/shard_map/ppermute | solution.py:17
  57.5 4.3 %collective-permute-start.12 = (f32[128,128]{0,1:T(8,128)S(1)}, f32[128,128]{0,1:T(8,128)S(1)}, u32[]{:S(2)}, u32[]{:S(2)}) collective-permute-start(f32[128,128]{0,1:T(8,128)S(1)} %add.149), channel_id=1, source_target_pairs={{0,4},{1,5},{2,6},{3,7},{4,0},{5,1},{6,2},{7,3},{8,12},{9,13},{10,... | collective-permute-start | bytes 196616 | tf_op jit(solution)/shard_map/ppermute | solution.py:17
  61.8 4.3 %collective-permute-start.13 = (f32[128,128]{0,1:T(8,128)S(1)}, f32[128,128]{0,1:T(8,128)S(1)}, u32[]{:S(2)}, u32[]{:S(2)}) collective-permute-start(f32[128,128]{0,1:T(8,128)S(1)} %add.150), channel_id=1, source_target_pairs={{0,2},{1,3},{2,0},{3,1},{4,6},{5,7},{6,4},{7,5},{8,10},{9,11},{10,... | collective-permute-start | bytes 196616 | tf_op jit(solution)/shard_map/ppermute | solution.py:17
  62.4 10.1 %collective-permute-start.17 = (f32[2,2,192,128]{3,2,1,0:T(8,128)S(1)}, f32[2,2,192,128]{3,2,1,0:T(8,128)S(1)}, u32[]{:S(2)}, u32[]{:S(2)}) collective-permute-start(f32[2,2,192,128]{3,2,1,0:T(8,128)S(1)} %dynamic-slice_bitcast_fusion), channel_id=1, source_target_pairs={{0,4},{1,5},{2,6},{3,7},{4,0},{5,1},{6,2},{7,3},{8,12},{9,13},{10,... | collective-permute-start | bytes 1179656 | tf_op jit(solution)/shard_map/ppermute | solution.py:17
  66.3 8.3 %collective-permute-start.15 = (f32[2,192,128]{2,1,0:T(8,128)S(1)}, f32[2,192,128]{2,1,0:T(8,128)S(1)}, u32[]{:S(2)}, u32[]{:S(2)}) collective-permute-start(f32[2,192,128]{2,1,0:T(8,128)S(1)} %dynamic-slice_bitcast_fusion.3), channel_id=1, source_target_pairs={{0,4},{1,5},{2,6},{3,7},{4,0},{5,1},{6,2},{7,3},{8,12},{9,13},{10,... | collective-permute-start | bytes 589832 | tf_op jit(solution)/shard_map/ppermute | solution.py:17
  72.7 5.7 %collective-permute-start.18 = (f32[2,192,128]{2,1,0:T(8,128)S(1)}, f32[2,192,128]{2,1,0:T(8,128)S(1)}, u32[]{:S(2)}, u32[]{:S(2)}) collective-permute-start(f32[2,192,128]{2,1,0:T(8,128)S(1)} %dynamic-slice_bitcast_fusion.2), channel_id=1, source_target_pairs={{0,2},{1,3},{2,0},{3,1},{4,6},{5,7},{6,4},{7,5},{8,10},{9,11},{10,... | collective-permute-start | bytes 589832 | tf_op jit(solution)/shard_map/ppermute | solution.py:17
  74.7 4.7 %collective-permute-start.16 = (f32[192,128]{1,0:T(8,128)S(1)}, f32[192,128]{1,0:T(8,128)S(1)}, u32[]{:S(2)}, u32[]{:S(2)}) collective-permute-start(f32[192,128]{1,0:T(8,128)S(1)} %dynamic-slice_bitcast_fusion.6), channel_id=1, source_target_pairs={{0,8},{1,9},{2,10},{3,11},{4,12},{5,13},{6,14},{7,15},{8,0},{9,1},... | collective-permute-start | bytes 294920 | tf_op jit(solution)/shard_map/ppermute | solution.py:17
  78.4 4.7 %collective-permute-start.19 = (f32[192,128]{1,0:T(8,128)S(1)}, f32[192,128]{1,0:T(8,128)S(1)}, u32[]{:S(2)}, u32[]{:S(2)}) collective-permute-start(f32[192,128]{1,0:T(8,128)S(1)} %dynamic-slice_bitcast_fusion.5), channel_id=1, source_target_pairs={{0,8},{1,9},{2,10},{3,11},{4,12},{5,13},{6,14},{7,15},{8,0},{9,1},... | collective-permute-start | bytes 294920 | tf_op jit(solution)/shard_map/ppermute | solution.py:17
  83.2 12.6 %collective-permute-start.20 = (f32[2,192,128]{2,1,0:T(8,128)S(1)}, f32[2,192,128]{2,1,0:T(8,128)S(1)}, u32[]{:S(2)}, u32[]{:S(2)}) collective-permute-start(f32[2,192,128]{2,1,0:T(8,128)S(1)} %pad_maximum_fusion.9), channel_id=1, source_target_pairs={{1,16},{3,18},{5,20},{7,22},{9,24},{11,26},{13,28},{15,30},{16,1},... | collective-permute-start | bytes 589832 | tf_op jit(solution)/shard_map/ppermute | solution.py:37
  95.8 4.7 %collective-permute-start.21 = (f32[192,128]{1,0:T(8,128)S(1)}, f32[192,128]{1,0:T(8,128)S(1)}, u32[]{:S(2)}, u32[]{:S(2)}) collective-permute-start(f32[192,128]{1,0:T(8,128)S(1)} %dynamic-slice_bitcast_fusion.4), channel_id=1, source_target_pairs={{0,1},{1,0},{2,3},{3,2},{4,5},{5,4},{6,7},{7,6},{8,9},{9,8},{10,11... | collective-permute-start | bytes 294920 | tf_op jit(solution)/shard_map/ppermute | solution.py:17
  101.0 1.3 %collective-permute-start.22 = (f32[128,128]{1,0:T(8,128)S(1)}, f32[128,128]{1,0:T(8,128)S(1)}, u32[]{:S(2)}, u32[]{:S(2)}) collective-permute-start(f32[128,128]{1,0:T(8,128)S(1)} %fusion.10), channel_id=1, source_target_pairs={{0,1},{1,0},{2,3},{3,2},{4,5},{5,4},{6,7},{7,6},{8,9},{9,8},{10,11... | collective-permute-start | bytes 196616 | tf_op jit(solution)/shard_map/ppermute | solution.py:17
  102.3 12.0 %collective-permute-start.23 = (f32[128,128]{1,0:T(8,128)S(1)}, f32[128,128]{1,0:T(8,128)S(1)}, u32[]{:S(2)}, u32[]{:S(2)}) collective-permute-start(f32[128,128]{1,0:T(8,128)S(1)} %add.168), channel_id=1, source_target_pairs={{0,2},{1,3},{2,0},{3,1},{4,6},{5,7},{6,4},{7,5},{8,10},{9,11},{10,... | collective-permute-start | bytes 196616 | tf_op jit(solution)/shard_map/ppermute | solution.py:17
  114.4 4.3 %collective-permute-start.24 = (f32[128,128]{1,0:T(8,128)S(1)}, f32[128,128]{1,0:T(8,128)S(1)}, u32[]{:S(2)}, u32[]{:S(2)}) collective-permute-start(f32[128,128]{1,0:T(8,128)S(1)} %add.169), channel_id=1, source_target_pairs={{0,4},{1,5},{2,6},{3,7},{4,0},{5,1},{6,2},{7,3},{8,12},{9,13},{10,... | collective-permute-start | bytes 196616 | tf_op jit(solution)/shard_map/ppermute | solution.py:17
  118.7 4.3 %collective-permute-start.25 = (f32[128,128]{1,0:T(8,128)S(1)}, f32[128,128]{1,0:T(8,128)S(1)}, u32[]{:S(2)}, u32[]{:S(2)}) collective-permute-start(f32[128,128]{1,0:T(8,128)S(1)} %add.170), channel_id=1, source_target_pairs={{0,8},{1,9},{2,10},{3,11},{4,12},{5,13},{6,14},{7,15},{8,0},{9,1},... | collective-permute-start | bytes 196616 | tf_op jit(solution)/shard_map/ppermute | solution.py:17
  123.0 5.2 %collective-permute-start.26 = (f32[128,128]{1,0:T(8,128)S(1)}, f32[128,128]{1,0:T(8,128)S(1)}, u32[]{:S(2)}, u32[]{:S(2)}) collective-permute-start(f32[128,128]{1,0:T(8,128)S(1)} %add.171), channel_id=1, source_target_pairs={{0,16},{1,17},{2,18},{3,19},{4,20},{5,21},{6,22},{7,23},{8,24},{9,... | collective-permute-start | bytes 196616 | tf_op jit(solution)/shard_map/ppermute | solution.py:17

commit v3 on v2

--- a/solution.py
+++ b/solution.py
@@ -1,6 +1,7 @@
 import jax
 import jax.numpy as jnp
 from jax import lax
+from jax.experimental import pallas as pl
 from jax.sharding import PartitionSpec as P
 
 HIGHEST = lax.Precision.HIGHEST
@@ -15,6 +16,53 @@
 
 def swap(x, s, n):
     return lax.ppermute(x, "pix", [(i, i ^ s) for i in range(n)])
+
+
+def invert_factor_kernel(gram_ref, out_ref):
+    rank = gram_ref.shape[0]
+    tiles = rank // 8
+    rows = lax.broadcasted_iota(jnp.int32, (8, rank), 0)
+    lanes = lax.broadcasted_iota(jnp.int32, (8, rank), 1)
+    a = [gram_ref[8 * t : 8 * t + 8, :] for t in range(tiles)]
+    b = [jnp.where(lanes == rows + 8 * t, 1.0, 0.0).astype(jnp.float32) for t in range(tiles)]
+
+    def spread(x):
+        return jnp.broadcast_to(x, (8, rank))
+
+    for t in range(tiles):
+        pivots = jnp.ones((8, rank), jnp.float32)
+        for r in range(0, 8, 2):
+            p = 8 * t + r
+            q = p + 1
+            app = spread(a[t][r : r + 1, p : p + 1])
+            apq = spread(a[t][r : r + 1, q : q + 1])
+            aqq = spread(a[t][r + 1 : r + 2, q : q + 1])
+            inv_p = 1.0 / app
+            step = apq * inv_p
+            left = aqq - apq * step
+            inv_q = 1.0 / left
+            pivots = jnp.where(rows == r, app, jnp.where(rows == r + 1, left, pivots))
+            row_p, row_q = spread(a[t][r : r + 1, :]), spread(a[t][r + 1 : r + 2, :])
+            row_q = row_q - step * row_p
+            low_p, low_q = spread(b[t][r : r + 1, :]), spread(b[t][r + 1 : r + 2, :])
+            low_q = low_q - step * low_p
+            for u in range(t, tiles):
+                col_p, col_q = spread(a[u][:, p : p + 1]), spread(a[u][:, q : q + 1])
+                f = col_p * inv_p
+                g = (col_q - f * apq) * inv_q
+                if u == t:
+                    f = jnp.where(rows > r, f, 0.0)
+                    g = jnp.where(rows > r + 1, g, 0.0)
+                b[u] = b[u] - f * low_p - g * low_q
+                if u > t or r < 6:
+                    a[u] = a[u] - f * row_p - g * row_q
+        out_ref[8 * t : 8 * t + 8, :] = b[t] * lax.rsqrt(pivots)
+
+
+def invert_factor(gram):
+    return pl.pallas_call(
+        invert_factor_kernel, out_shape=jax.ShapeDtypeStruct(gram.shape, jnp.float32)
+    )(gram)
 
 
 def body(green, sketch):
@@ -92,14 +140,13 @@
             scatter(partial[..., 1, :, :], order_b[::-1]),
         ]
     )
-    sums = jnp.where(own_half, sums, cross(sums))
-    raw = lax.dynamic_index_in_dim(sums, core, 0, False) + swap(
-        lax.dynamic_index_in_dim(sums, 1 - core, 0, False), 1, n
-    )
-    raw_gram = total(dot(raw, raw, ((0,), (0,))), [1] + middle + [top])
+    sums = sums + swap(sums, top, n)
+    summed = sums.reshape(2 * rows, rank)
+    raw_gram = total(dot(summed, summed, ((0,), (0,))), [1] + middle)
+    handed = swap(lax.dynamic_index_in_dim(sums, 1 - core, 0, False), 1, n)
+    raw = jnp.where(own_half, lax.dynamic_index_in_dim(sums, core, 0, False), handed)
 
-    lower = jnp.linalg.cholesky(gram)
-    inverse = jax.scipy.linalg.solve_triangular(lower, jnp.eye(rank, dtype=jnp.float32), lower=True)
+    inverse = invert_factor(gram)
     mine = lax.dynamic_slice_in_dim(sketched, core * pixels, pixels, 0)
     basis = jnp.sqrt(jnp.float32(pixels * n)) * dot(mine, inverse, ((1,), (1,)))
     projection = dot(raw, inverse, ((1,), (1,)))

time: 130 us -> 114 us (0.88)
  other arithmetic: 25.9 us -> 3.67 us
  Pallas kernels: 0 us -> 10.5 us
  waiting for transfers between devices: 61 us -> 53.3 us
  matrix products: 6.25 us -> 8.56 us
    another operation x5 -> x0, other arithmetic: 22.8 us -> none  [the longest x3 12.4 us: body(): lower = jnp.linalg.cholesky(gram)]
    pallas_call x0 -> x1, Pallas kernels: none -> 10.5 us  [invert_factor(): pl.pallas_call(invert_factor_kernel, out_shape=jax.ShapeDtypeStruct(gram....]
    ppermute x25, waiting for transfers between devices: 61 us -> 53.3 us  [swap(): return lax.ppermute(x, 'pix', [(i, i ^ s) for i in range(n)])]
    dot_general x8, matrix products: 6 us -> 8.56 us  [dot(): lax.dot_general(a, b, (contract, ((), ())), precision=precision, preferre...]
    ppermute x25, starting transfers between devices: 33.2 us -> 35.1 us  [swap(): return lax.ppermute(x, 'pix', [(i, i ^ s) for i in range(n)])]
  transfers between devices with their start and end apart: 27 -> 26, of which waited for: 20 -> 18; matrix products, arithmetic and copies ran while one was open for 21% -> 6% of each run, Pallas kernels for 0% -> 9%
where the time goes in v3:
time: 114 us; the launch traced here: 113 us
  waiting for transfers between devices  53.3 us (47%)
  starting transfers between devices  35.7 us (31%)
  Pallas kernels  10.5 us (9%)
  matrix products  8.56 us (8%)
  other arithmetic  3.67 us (3%)
    ppermute x25, waiting for transfers between devices, swap(): return lax.ppermute(x, 'pix', [(i, i ^ s) for i in range(n)])  53.3 us
    ppermute x25, starting transfers between devices, swap(): return lax.ppermute(x, 'pix', [(i, i ^ s) for i in range(n)])  35.1 us
    pallas_call x1, Pallas kernels, invert_factor(): pl.pallas_call(invert_factor_kernel, out_shape=jax.ShapeDtypeStruct(gram....  10.5 us
    dot_general x8, matrix products, dot(): lax.dot_general(a, b, (contract, ((), ())), precision=precision, preferre...  8.56 us
  transfers between devices with their start and end apart: 26, of which 18 were waited for; matrix products, arithmetic and copies ran while one was open for 6% of the time, Pallas kernels for 9%

profile of v3, /device:TPU:0, one launch (start us, length us, event | category | flops | bytes accessed | tf_op | source)
XLA Modules:
  0.0 113.1 jit_solution(6721756501900839425)
XLA Ops:
  0.6 0.6 collective-permute-start.1
  1.2 1.2 %collective-permute-done.1 = f32[192,128]{1,0:T(8,128)S(1)} collective-permute-done((f32[192,128]{1,0:T(8,128)}, f32[192,128]{1,0:T(8,128)S(1)}, u32[]{:S(2)}, u32[]{:S(2)}) %collective-permute-start.1) | collective-permute-done | bytes 98336 | tf_op jit(solution)/shard_map/ppermute | solution.py:18
  2.4 0.9 select_bitcast_fusion.13
  3.3 0.7 collective-permute-start.2
  4.1 3.0 %collective-permute-start.3 = (f32[192,128]{1,0:T(8,128)S(1)}, f32[192,128]{1,0:T(8,128)S(1)}, u32[]{:S(2)}, u32[]{:S(2)}) collective-permute-start(f32[192,128]{1,0:T(8,128)S(1)} %get-tuple-element.21), channel_id=1, source_target_pairs={{0,8},{1,9},{2,10},{3,11},{4,12},{5,13},{6,14},{7,15},{8,0},{9,1},... | collective-permute-start | bytes 294920 | tf_op jit(solution)/shard_map/ppermute | solution.py:18
  7.1 2.5 %collective-permute-done.3 = f32[192,128]{1,0:T(8,128)S(1)} collective-permute-done((f32[192,128]{1,0:T(8,128)S(1)}, f32[192,128]{1,0:T(8,128)S(1)}, u32[]{:S(2)}, u32[]{:S(2)}) %collective-permute-start.3) | collective-permute-done | bytes 98336 | tf_op jit(solution)/shard_map/ppermute | solution.py:18
  9.6 4.0 %collective-permute-done.6 = f32[192,128]{1,0:T(8,128)S(1)} collective-permute-done((f32[192,128]{1,0:T(8,128)S(1)}, f32[192,128]{1,0:T(8,128)S(1)}, u32[]{:S(2)}, u32[]{:S(2)}) %collective-permute-start.6) | collective-permute-done | bytes 98336 | tf_op jit(solution)/shard_map/ppermute | solution.py:18
  13.7 1.5 %collective-permute-start.4 = (f32[2,192,128]{2,1,0:T(8,128)S(1)}, f32[2,192,128]{2,1,0:T(8,128)S(1)}, u32[]{:S(2)}, u32[]{:S(2)}) collective-permute-start(f32[2,192,128]{2,1,0:T(8,128)S(1)} %pad_maximum_fusion.7), channel_id=1, source_target_pairs={{0,4},{1,5},{2,6},{3,7},{4,0},{5,1},{6,2},{7,3},{8,12},{9,13},{10,... | collective-permute-start | bytes 589832 | tf_op jit(solution)/shard_map/ppermute | solution.py:18
  15.3 5.7 %collective-permute-start = (f32[64,3072]{1,0:T(8,128)S(1)}, f32[64,3072]{1,0:T(8,128)}, u32[]{:S(2)}, u32[]{:S(2)}) collective-permute-start(f32[64,3072]{1,0:T(8,128)S(1)} %slice_select_fusion), channel_id=1, source_target_pairs={{0,1},{1,0},{2,3},{3,2},{4,5},{5,4},{6,7},{7,6},{8,9},{9,8},{10,11... | collective-permute-start | bytes 2359304 | tf_op jit(solution)/shard_map/ppermute | solution.py:18
  21.0 1.6 %collective-permute-start.7 = (f32[2,192,128]{2,1,0:T(8,128)S(1)}, f32[2,192,128]{2,1,0:T(8,128)S(1)}, u32[]{:S(2)}, u32[]{:S(2)}) collective-permute-start(f32[2,192,128]{2,1,0:T(8,128)S(1)} %pad_maximum_fusion.8), channel_id=1, source_target_pairs={{0,2},{1,3},{2,0},{3,1},{4,6},{5,7},{6,4},{7,5},{8,10},{9,11},{10,... | collective-permute-start | bytes 589832 | tf_op jit(solution)/shard_map/ppermute | solution.py:18
  22.6 0.6 collective-permute-start.5
  23.2 5.6 %collective-permute-done.7 = f32[2,192,128]{2,1,0:T(8,128)S(1)} collective-permute-done((f32[2,192,128]{2,1,0:T(8,128)S(1)}, f32[2,192,128]{2,1,0:T(8,128)S(1)}, u32[]{:S(2)}, u32[]{:S(2)}) %collective-permute-start.7) | collective-permute-done | bytes 196640 | tf_op jit(solution)/shard_map/ppermute | solution.py:18
  29.0 1.3 %broadcast_select_fusion.1 = (f32[64,3072]{1,0:T(8,128)S(1)}, f32[64,3072]{1,0:T(8,128)S(1)}) fusion(f32[64,3072]{1,0:T(8,128)} %collective-permute-done, pred[]{:T(512)S(6)} %eq.55, f32[64,6144]{1,0:T(8,128)S(1)} %copy-done), kind=kLoop, calls=%fused_computation.22 | loop fusion | flops 589824 | bytes 3932161 | tf_op jit(solution)/shard_map/jit(_where)/select_n | solution.py:128
  30.3 8.0 %collective-permute-done.8 = f32[2,2,192,128]{3,2,1,0:T(8,128)S(1)} collective-permute-done((f32[2,2,192,128]{3,2,1,0:T(8,128)S(1)}, f32[2,2,192,128]{3,2,1,0:T(8,128)S(1)}, u32[]{:S(2)}, u32[]{:S(2)}) %collective-permute-start.8) | collective-permute-done | bytes 393248 | tf_op jit(solution)/shard_map/ppermute | solution.py:18
  38.6 1.0 fusion.1
  39.7 1.2 %collective-permute-done.9 = f32[128,128]{1,0:T(8,128)S(1)} collective-permute-done((f32[128,128]{1,0:T(8,128)S(1)}, f32[128,128]{1,0:T(8,128)S(1)}, u32[]{:S(2)}, u32[]{:S(2)}) %collective-permute-start.9) | collective-permute-done | bytes 65568 | tf_op jit(solution)/shard_map/ppermute | solution.py:18
  41.0 1.4 %fusion = f32[3072,128]{1,0:T(8,128)S(1)} fusion(f32[128,128]{1,0:T(8,128)S(1)} %add.131, f32[64,3072]{1,0:T(8,128)S(1)} %get-tuple-element.4, f32[64,3072]{1,0:T(8,128)S(1)} %get-tuple-element.3), kind=kOutput, calls=%fused_computation.2 | convolution fusion | flops 302383104 | bytes 3211264 | tf_op jit(solution)/shard_map/dot_general | solution.py:12
  42.6 1.6 %collective-permute-start.14 = (f32[2,2,192,128]{3,2,1,0:T(8,128)S(1)}, f32[2,2,192,128]{3,2,1,0:T(8,128)S(1)}, u32[]{:S(2)}, u32[]{:S(2)}) collective-permute-start(f32[2,2,192,128]{3,2,1,0:T(8,128)S(1)} %dynamic-slice_bitcast_fusion.1), channel_id=1, source_target_pairs={{0,2},{1,3},{2,0},{3,1},{4,6},{5,7},{6,4},{7,5},{8,10},{9,11},{10,... | collective-permute-start | bytes 1179656 | tf_op jit(solution)/shard_map/ppermute | solution.py:18
  44.2 0.6 collective-permute-start.17
  44.7 0.3 fusion.16
  45.0 5.1 %collective-permute-start.10 = (f32[128,128]{1,0:T(8,128)S(1)}, f32[128,128]{1,0:T(8,128)S(1)}, u32[]{:S(2)}, u32[]{:S(2)}) collective-permute-start(f32[128,128]{1,0:T(8,128)S(1)} %fusion.16), channel_id=1, source_target_pairs={{0,16},{1,17},{2,18},{3,19},{4,20},{5,21},{6,22},{7,23},{8,24},{9,... | collective-permute-start | bytes 196616 | tf_op jit(solution)/shard_map/ppermute | solution.py:18
  50.2 3.7 %collective-permute-done.14 = f32[2,2,192,128]{3,2,1,0:T(8,128)S(1)} collective-permute-done((f32[2,2,192,128]{3,2,1,0:T(8,128)S(1)}, f32[2,2,192,128]{3,2,1,0:T(8,128)S(1)}, u32[]{:S(2)}, u32[]{:S(2)}) %collective-permute-start.14) | collective-permute-done | bytes 393248 | tf_op jit(solution)/shard_map/ppermute | solution.py:18
  53.9 0.7 collective-permute-start.15
  54.6 0.6 collective-permute-done.17
  55.2 0.9 collective-permute-start.18
  56.1 4.0 %collective-permute-done.15 = f32[2,192,128]{2,1,0:T(8,128)S(1)} collective-permute-done((f32[2,192,128]{2,1,0:T(8,128)S(1)}, f32[2,192,128]{2,1,0:T(8,128)S(1)}, u32[]{:S(2)}, u32[]{:S(2)}) %collective-permute-start.15) | collective-permute-done | bytes 196640 | tf_op jit(solution)/shard_map/ppermute | solution.py:18
  60.1 0.8 collective-permute-start.16
  61.2 1.2 %collective-permute-start.19 = (f32[192,128]{1,0:T(8,128)S(1)}, f32[192,128]{1,0:T(8,128)S(1)}, u32[]{:S(2)}, u32[]{:S(2)}) collective-permute-start(f32[192,128]{1,0:T(8,128)S(1)} %dynamic-slice_bitcast_fusion.5), channel_id=1, source_target_pairs={{0,8},{1,9},{2,10},{3,11},{4,12},{5,13},{6,14},{7,15},{8,0},{9,1},... | collective-permute-start | bytes 294920 | tf_op jit(solution)/shard_map/ppermute | solution.py:18
  62.3 2.5 %collective-permute-done.16 = f32[192,128]{1,0:T(8,128)S(1)} collective-permute-done((f32[192,128]{1,0:T(8,128)S(1)}, f32[192,128]{1,0:T(8,128)S(1)}, u32[]{:S(2)}, u32[]{:S(2)}) %collective-permute-start.16) | collective-permute-done | bytes 98336 | tf_op jit(solution)/shard_map/ppermute | solution.py:18
  64.8 1.0 collective-permute-done.19
  65.9 6.1 %collective-permute-start.20 = (f32[2,192,128]{2,1,0:T(8,128)S(1)}, f32[2,192,128]{2,1,0:T(8,128)S(1)}, u32[]{:S(2)}, u32[]{:S(2)}) collective-permute-start(f32[2,192,128]{2,1,0:T(8,128)S(1)} %pad_maximum_fusion.9), channel_id=1, source_target_pairs={{0,16},{1,17},{2,18},{3,19},{4,20},{5,21},{6,22},{7,23},{8,24},{9,... | collective-permute-start | bytes 589832 | tf_op jit(solution)/shard_map/ppermute | solution.py:18
  72.2 6.1 %collective-permute-done.11 = f32[128,128]{1,0:T(8,128)S(1)} collective-permute-done((f32[128,128]{1,0:T(8,128)S(1)}, f32[128,128]{1,0:T(8,128)S(1)}, u32[]{:S(2)}, u32[]{:S(2)}) %collective-permute-start.11) | collective-permute-done | bytes 65568 | tf_op jit(solution)/shard_map/ppermute | solution.py:18
  78.3 0.8 collective-permute-start.12
  79.1 3.6 %collective-permute-done.12 = f32[128,128]{1,0:T(8,128)S(1)} collective-permute-done((f32[128,128]{1,0:T(8,128)S(1)}, f32[128,128]{1,0:T(8,128)S(1)}, u32[]{:S(2)}, u32[]{:S(2)}) %collective-permute-start.12) | collective-permute-done | bytes 65568 | tf_op jit(solution)/shard_map/ppermute | solution.py:18
  82.7 1.6 %collective-permute-start.13 = (f32[128,128]{1,0:T(8,128)S(1)}, f32[128,128]{1,0:T(8,128)S(1)}, u32[]{:S(2)}, u32[]{:S(2)}) collective-permute-start(f32[128,128]{1,0:T(8,128)S(1)} %add.135), channel_id=1, source_target_pairs={{0,2},{1,3},{2,0},{3,1},{4,6},{5,7},{6,4},{7,5},{8,10},{9,11},{10,... | collective-permute-start | bytes 196616 | tf_op jit(solution)/shard_map/ppermute | solution.py:18
  84.3 0.5 convolution_bitcast_fusion
  84.8 2.2 %collective-permute-done.13 = f32[128,128]{1,0:T(8,128)S(1)} collective-permute-done((f32[128,128]{1,0:T(8,128)S(1)}, f32[128,128]{1,0:T(8,128)S(1)}, u32[]{:S(2)}, u32[]{:S(2)}) %collective-permute-start.13) | collective-permute-done | bytes 65568 | tf_op jit(solution)/shard_map/ppermute | solution.py:18
  87.0 0.6 add.136.gram_ref
  87.6 10.5 %shard_map.49 = f32[128,128]{1,0:T(8,128)} custom-call(f32[128,128]{1,0:T(8,128)} %add.136.gram_ref), custom_call_target="tpu_custom_call" | custom-call | tf_op jit(solution)/shard_map/pallas_call | solution.py:63
  98.2 1.6 %collective-permute-start.23 = (f32[128,128]{1,0:T(8,128)S(1)}, f32[128,128]{1,0:T(8,128)S(1)}, u32[]{:S(2)}, u32[]{:S(2)}) collective-permute-start(f32[128,128]{1,0:T(8,128)S(1)} %add.152), channel_id=1, source_target_pairs={{0,2},{1,3},{2,0},{3,1},{4,6},{5,7},{6,4},{7,5},{8,10},{9,11},{10,... | collective-permute-start | bytes 196616 | tf_op jit(solution)/shard_map/ppermute | solution.py:18
  99.8 2.7 %collective-permute-done.23 = f32[128,128]{1,0:T(8,128)S(1)} collective-permute-done((f32[128,128]{1,0:T(8,128)S(1)}, f32[128,128]{1,0:T(8,128)S(1)}, u32[]{:S(2)}, u32[]{:S(2)}) %collective-permute-start.23) | collective-permute-done | bytes 65568 | tf_op jit(solution)/shard_map/ppermute | solution.py:18
  102.5 0.8 collective-permute-start.24
  103.3 1.7 %convolution_multiply_fusion.1 = f32[64,128]{1,0:T(8,128)} fusion(f32[128,128]{1,0:T(8,128)} %shard_map.49, f32[128,128]{1,0:T(8,128)S(1)} %add.131, s32[]{:T(128)S(6)} %select_n.273), kind=kOutput, calls=%fused_computation.6 | convolution fusion | flops 12591104 | bytes 131076 | tf_op jit(solution)/shard_map/dot_general | solution.py:12
  105.0 1.9 %collective-permute-done.24 = f32[128,128]{1,0:T(8,128)S(1)} collective-permute-done((f32[128,128]{1,0:T(8,128)S(1)}, f32[128,128]{1,0:T(8,128)S(1)}, u32[]{:S(2)}, u32[]{:S(2)}) %collective-permute-start.24) | collective-permute-done | bytes 65568 | tf_op jit(solution)/shard_map/ppermute | solution.py:18
  107.0 1.8 %fusion.2 = f32[192,128]{1,0:T(8,128)} fusion(f32[128,128]{1,0:T(8,128)} %shard_map.49, f32[192,128]{1,0:T(8,128)S(1)} %collective-permute-done.21, f32[2,192,128]{2,1,0:T(8,128)S(1)} %fusion.14, s32[]{:T(128)S(6)} %select_n.281, pred[]{:T(512)S(6)} %eq.59), kind=kOutput, calls=%fused_computation.38 | convolution fusion | flops 37773312 | bytes 360453 | tf_op jit(solution)/shard_map/dot_general | solution.py:12
  108.7 2.4 %collective-permute-done.25 = f32[128,128]{1,0:T(8,128)S(1)} collective-permute-done((f32[128,128]{1,0:T(8,128)S(1)}, f32[128,128]{1,0:T(8,128)S(1)}, u32[]{:S(2)}, u32[]{:S(2)}) %collective-permute-start.25) | collective-permute-done | bytes 65568 | tf_op jit(solution)/shard_map/ppermute | solution.py:18
  111.2 1.0 fusion.6
  112.2 0.9 convolution_multiply_fusion
  (58 shorter events, 2.1 us)
Async XLA Ops:
  0.6 14.6 %copy-start = (f32[64,6144]{1,0:T(8,128)S(1)}, f32[64,6144]{1,0:T(8,128)}, u32[]{:S(2)}) copy-start(f32[64,6144]{1,0:T(8,128)} %param.2) | copy-start | bytes 4718596
  0.6 1.7 %collective-permute-start.1 = (f32[192,128]{1,0:T(8,128)}, f32[192,128]{1,0:T(8,128)S(1)}, u32[]{:S(2)}, u32[]{:S(2)}) collective-permute-start(f32[192,128]{1,0:T(8,128)} %param.3), channel_id=1, source_target_pairs={{0,1},{1,0},{2,3},{3,2},{4,5},{5,4},{6,7},{7,6},{8,9},{9,8},{10,11... | collective-permute-start | bytes 294920 | tf_op jit(solution)/shard_map/ppermute | solution.py:18
  3.3 0.7 collective-permute-start.2
  4.1 5.6 %collective-permute-start.3 = (f32[192,128]{1,0:T(8,128)S(1)}, f32[192,128]{1,0:T(8,128)S(1)}, u32[]{:S(2)}, u32[]{:S(2)}) collective-permute-start(f32[192,128]{1,0:T(8,128)S(1)} %get-tuple-element.21), channel_id=1, source_target_pairs={{0,8},{1,9},{2,10},{3,11},{4,12},{5,13},{6,14},{7,15},{8,0},{9,1},... | collective-permute-start | bytes 294920 | tf_op jit(solution)/shard_map/ppermute | solution.py:18
  7.0 6.6 %collective-permute-start.6 = (f32[192,128]{1,0:T(8,128)S(1)}, f32[192,128]{1,0:T(8,128)S(1)}, u32[]{:S(2)}, u32[]{:S(2)}) collective-permute-start(f32[192,128]{1,0:T(8,128)S(1)} %get-tuple-element.22), channel_id=1, source_target_pairs={{0,8},{1,9},{2,10},{3,11},{4,12},{5,13},{6,14},{7,15},{8,0},{9,1},... | collective-permute-start | bytes 294920 | tf_op jit(solution)/shard_map/ppermute | solution.py:18
  13.7 8.9 %collective-permute-start.4 = (f32[2,192,128]{2,1,0:T(8,128)S(1)}, f32[2,192,128]{2,1,0:T(8,128)S(1)}, u32[]{:S(2)}, u32[]{:S(2)}) collective-permute-start(f32[2,192,128]{2,1,0:T(8,128)S(1)} %pad_maximum_fusion.7), channel_id=1, source_target_pairs={{0,4},{1,5},{2,6},{3,7},{4,0},{5,1},{6,2},{7,3},{8,12},{9,13},{10,... | collective-permute-start | bytes 589832 | tf_op jit(solution)/shard_map/ppermute | solution.py:18
  15.3 13.7 %collective-permute-start = (f32[64,3072]{1,0:T(8,128)S(1)}, f32[64,3072]{1,0:T(8,128)}, u32[]{:S(2)}, u32[]{:S(2)}) collective-permute-start(f32[64,3072]{1,0:T(8,128)S(1)} %slice_select_fusion), channel_id=1, source_target_pairs={{0,1},{1,0},{2,3},{3,2},{4,5},{5,4},{6,7},{7,6},{8,9},{9,8},{10,11... | collective-permute-start | bytes 2359304 | tf_op jit(solution)/shard_map/ppermute | solution.py:18
  21.0 7.8 %collective-permute-start.7 = (f32[2,192,128]{2,1,0:T(8,128)S(1)}, f32[2,192,128]{2,1,0:T(8,128)S(1)}, u32[]{:S(2)}, u32[]{:S(2)}) collective-permute-start(f32[2,192,128]{2,1,0:T(8,128)S(1)} %pad_maximum_fusion.8), channel_id=1, source_target_pairs={{0,2},{1,3},{2,0},{3,1},{4,6},{5,7},{6,4},{7,5},{8,10},{9,11},{10,... | collective-permute-start | bytes 589832 | tf_op jit(solution)/shard_map/ppermute | solution.py:18
  22.6 15.8 %collective-permute-start.5 = (f32[2,2,192,128]{3,2,0,1:T(8,128)S(1)}, f32[2,2,192,128]{3,2,0,1:T(8,128)S(1)}, u32[]{:S(2)}, u32[]{:S(2)}) collective-permute-start(f32[2,2,192,128]{3,2,0,1:T(8,128)S(1)} %pad_maximum_fusion.4), channel_id=1, source_target_pairs={{0,2},{1,3},{2,0},{3,1},{4,6},{5,7},{6,4},{7,5},{8,10},{9,11},{10,... | collective-permute-start | bytes 1179656 | tf_op jit(solution)/shard_map/ppermute | solution.py:18
  28.9 9.4 %collective-permute-start.8 = (f32[2,2,192,128]{3,2,1,0:T(8,128)S(1)}, f32[2,2,192,128]{3,2,1,0:T(8,128)S(1)}, u32[]{:S(2)}, u32[]{:S(2)}) collective-permute-start(f32[2,2,192,128]{3,2,1,0:T(8,128)S(1)} %pad_maximum_fusion.5), channel_id=1, source_target_pairs={{0,4},{1,5},{2,6},{3,7},{4,0},{5,1},{6,2},{7,3},{8,12},{9,13},{10,... | collective-permute-start | bytes 1179656 | tf_op jit(solution)/shard_map/ppermute | solution.py:18
  39.6 1.3 %collective-permute-start.9 = (f32[128,128]{1,0:T(8,128)S(1)}, f32[128,128]{1,0:T(8,128)S(1)}, u32[]{:S(2)}, u32[]{:S(2)}) collective-permute-start(f32[128,128]{1,0:T(8,128)S(1)} %fusion.1), channel_id=1, source_target_pairs={{0,1},{1,0},{2,3},{3,2},{4,5},{5,4},{6,7},{7,6},{8,9},{9,8},{10,11... | collective-permute-start | bytes 196616 | tf_op jit(solution)/shard_map/ppermute | solution.py:18
  42.6 11.2 %collective-permute-start.14 = (f32[2,2,192,128]{3,2,1,0:T(8,128)S(1)}, f32[2,2,192,128]{3,2,1,0:T(8,128)S(1)}, u32[]{:S(2)}, u32[]{:S(2)}) collective-permute-start(f32[2,2,192,128]{3,2,1,0:T(8,128)S(1)} %dynamic-slice_bitcast_fusion.1), channel_id=1, source_target_pairs={{0,2},{1,3},{2,0},{3,1},{4,6},{5,7},{6,4},{7,5},{8,10},{9,11},{10,... | collective-permute-start | bytes 1179656 | tf_op jit(solution)/shard_map/ppermute | solution.py:18
  44.2 11.0 %collective-permute-start.17 = (f32[2,2,192,128]{3,2,1,0:T(8,128)S(1)}, f32[2,2,192,128]{3,2,1,0:T(8,128)S(1)}, u32[]{:S(2)}, u32[]{:S(2)}) collective-permute-start(f32[2,2,192,128]{3,2,1,0:T(8,128)S(1)} %dynamic-slice_bitcast_fusion), channel_id=1, source_target_pairs={{0,4},{1,5},{2,6},{3,7},{4,0},{5,1},{6,2},{7,3},{8,12},{9,13},{10,... | collective-permute-start | bytes 1179656 | tf_op jit(solution)/shard_map/ppermute | solution.py:18
  45.0 26.9 %collective-permute-start.10 = (f32[128,128]{1,0:T(8,128)S(1)}, f32[128,128]{1,0:T(8,128)S(1)}, u32[]{:S(2)}, u32[]{:S(2)}) collective-permute-start(f32[128,128]{1,0:T(8,128)S(1)} %fusion.16), channel_id=1, source_target_pairs={{0,16},{1,17},{2,18},{3,19},{4,20},{5,21},{6,22},{7,23},{8,24},{9,... | collective-permute-start | bytes 196616 | tf_op jit(solution)/shard_map/ppermute | solution.py:18
  53.9 6.2 %collective-permute-start.15 = (f32[2,192,128]{2,1,0:T(8,128)S(1)}, f32[2,192,128]{2,1,0:T(8,128)S(1)}, u32[]{:S(2)}, u32[]{:S(2)}) collective-permute-start(f32[2,192,128]{2,1,0:T(8,128)S(1)} %dynamic-slice_bitcast_fusion.3), channel_id=1, source_target_pairs={{0,4},{1,5},{2,6},{3,7},{4,0},{5,1},{6,2},{7,3},{8,12},{9,13},{10,... | collective-permute-start | bytes 589832 | tf_op jit(solution)/shard_map/ppermute | solution.py:18
  55.2 5.9 %collective-permute-start.18 = (f32[2,192,128]{2,1,0:T(8,128)S(1)}, f32[2,192,128]{2,1,0:T(8,128)S(1)}, u32[]{:S(2)}, u32[]{:S(2)}) collective-permute-start(f32[2,192,128]{2,1,0:T(8,128)S(1)} %dynamic-slice_bitcast_fusion.2), channel_id=1, source_target_pairs={{0,2},{1,3},{2,0},{3,1},{4,6},{5,7},{6,4},{7,5},{8,10},{9,11},{10,... | collective-permute-start | bytes 589832 | tf_op jit(solution)/shard_map/ppermute | solution.py:18
  60.1 4.7 %collective-permute-start.16 = (f32[192,128]{1,0:T(8,128)S(1)}, f32[192,128]{1,0:T(8,128)S(1)}, u32[]{:S(2)}, u32[]{:S(2)}) collective-permute-start(f32[192,128]{1,0:T(8,128)S(1)} %dynamic-slice_bitcast_fusion.6), channel_id=1, source_target_pairs={{0,8},{1,9},{2,10},{3,11},{4,12},{5,13},{6,14},{7,15},{8,0},{9,1},... | collective-permute-start | bytes 294920 | tf_op jit(solution)/shard_map/ppermute | solution.py:18
  61.2 4.7 %collective-permute-start.19 = (f32[192,128]{1,0:T(8,128)S(1)}, f32[192,128]{1,0:T(8,128)S(1)}, u32[]{:S(2)}, u32[]{:S(2)}) collective-permute-start(f32[192,128]{1,0:T(8,128)S(1)} %dynamic-slice_bitcast_fusion.5), channel_id=1, source_target_pairs={{0,8},{1,9},{2,10},{3,11},{4,12},{5,13},{6,14},{7,15},{8,0},{9,1},... | collective-permute-start | bytes 294920 | tf_op jit(solution)/shard_map/ppermute | solution.py:18
  65.9 18.3 %collective-permute-start.20 = (f32[2,192,128]{2,1,0:T(8,128)S(1)}, f32[2,192,128]{2,1,0:T(8,128)S(1)}, u32[]{:S(2)}, u32[]{:S(2)}) collective-permute-start(f32[2,192,128]{2,1,0:T(8,128)S(1)} %pad_maximum_fusion.9), channel_id=1, source_target_pairs={{0,16},{1,17},{2,18},{3,19},{4,20},{5,21},{6,22},{7,23},{8,24},{9,... | collective-permute-start | bytes 589832 | tf_op jit(solution)/shard_map/ppermute | solution.py:18
  72.0 6.3 %collective-permute-start.11 = (f32[128,128]{1,0:T(8,128)S(1)}, f32[128,128]{1,0:T(8,128)S(1)}, u32[]{:S(2)}, u32[]{:S(2)}) collective-permute-start(f32[128,128]{1,0:T(8,128)S(1)} %add.133), channel_id=1, source_target_pairs={{0,8},{1,9},{2,10},{3,11},{4,12},{5,13},{6,14},{7,15},{8,0},{9,1},... | collective-permute-start | bytes 196616 | tf_op jit(solution)/shard_map/ppermute | solution.py:18
  78.3 4.3 %collective-permute-start.12 = (f32[128,128]{1,0:T(8,128)S(1)}, f32[128,128]{1,0:T(8,128)S(1)}, u32[]{:S(2)}, u32[]{:S(2)}) collective-permute-start(f32[128,128]{1,0:T(8,128)S(1)} %add.134), channel_id=1, source_target_pairs={{0,4},{1,5},{2,6},{3,7},{4,0},{5,1},{6,2},{7,3},{8,12},{9,13},{10,... | collective-permute-start | bytes 196616 | tf_op jit(solution)/shard_map/ppermute | solution.py:18
  82.7 4.3 %collective-permute-start.13 = (f32[128,128]{1,0:T(8,128)S(1)}, f32[128,128]{1,0:T(8,128)S(1)}, u32[]{:S(2)}, u32[]{:S(2)}) collective-permute-start(f32[128,128]{1,0:T(8,128)S(1)} %add.135), channel_id=1, source_target_pairs={{0,2},{1,3},{2,0},{3,1},{4,6},{5,7},{6,4},{7,5},{8,10},{9,11},{10,... | collective-permute-start | bytes 196616 | tf_op jit(solution)/shard_map/ppermute | solution.py:18
  84.7 13.4 %collective-permute-start.22 = (f32[128,128]{1,0:T(8,128)S(1)}, f32[128,128]{1,0:T(8,128)S(1)}, u32[]{:S(2)}, u32[]{:S(2)}) collective-permute-start(f32[128,128]{1,0:T(8,128)S(1)} %convolution_bitcast_fusion), channel_id=1, source_target_pairs={{0,1},{1,0},{2,3},{3,2},{4,5},{5,4},{6,7},{7,6},{8,9},{9,8},{10,11... | collective-permute-start | bytes 196616 | tf_op jit(solution)/shard_map/ppermute | solution.py:18
  98.1 14.1 %copy-start.1 = (f32[128,128]{1,0:T(8,128)S(1)}, f32[128,128]{1,0:T(8,128)}, u32[]{:S(2)}) copy-start(f32[128,128]{1,0:T(8,128)} %shard_map.49) | copy-start | bytes 196612
  98.2 4.3 %collective-permute-start.23 = (f32[128,128]{1,0:T(8,128)S(1)}, f32[128,128]{1,0:T(8,128)S(1)}, u32[]{:S(2)}, u32[]{:S(2)}) collective-permute-start(f32[128,128]{1,0:T(8,128)S(1)} %add.152), channel_id=1, source_target_pairs={{0,2},{1,3},{2,0},{3,1},{4,6},{5,7},{6,4},{7,5},{8,10},{9,11},{10,... | collective-permute-start | bytes 196616 | tf_op jit(solution)/shard_map/ppermute | solution.py:18
  99.7 7.3 %collective-permute-start.21 = (f32[192,128]{1,0:T(8,128)S(1)}, f32[192,128]{1,0:T(8,128)S(1)}, u32[]{:S(2)}, u32[]{:S(2)}) collective-permute-start(f32[192,128]{1,0:T(8,128)S(1)} %dynamic-slice_bitcast_fusion.4), channel_id=1, source_target_pairs={{0,1},{1,0},{2,3},{3,2},{4,5},{5,4},{6,7},{7,6},{8,9},{9,8},{10,11... | collective-permute-start | bytes 294920 | tf_op jit(solution)/shard_map/ppermute | solution.py:18
  102.5 4.3 %collective-permute-start.24 = (f32[128,128]{1,0:T(8,128)S(1)}, f32[128,128]{1,0:T(8,128)S(1)}, u32[]{:S(2)}, u32[]{:S(2)}) collective-permute-start(f32[128,128]{1,0:T(8,128)S(1)} %add.153), channel_id=1, source_target_pairs={{0,4},{1,5},{2,6},{3,7},{4,0},{5,1},{6,2},{7,3},{8,12},{9,13},{10,... | collective-permute-start | bytes 196616 | tf_op jit(solution)/shard_map/ppermute | solution.py:18
  106.8 4.3 %collective-permute-start.25 = (f32[128,128]{1,0:T(8,128)S(1)}, f32[128,128]{1,0:T(8,128)S(1)}, u32[]{:S(2)}, u32[]{:S(2)}) collective-permute-start(f32[128,128]{1,0:T(8,128)S(1)} %add.154), channel_id=1, source_target_pairs={{0,8},{1,9},{2,10},{3,11},{4,12},{5,13},{6,14},{7,15},{8,0},{9,1},... | collective-permute-start | bytes 196616 | tf_op jit(solution)/shard_map/ppermute | solution.py:18
